TPU v7x, 128 devices: a whole 4x4x4 slice. The times are simulated.
128 devices in a mesh: rows: 64 (over z, y, x), terms: 2 (over core).
Axes of the slice: x: 4, y: 4, z: 4, core: 2. Of those that a mesh axis runs over, the one named last changes fastest.
Arguments:
- wavefunc: float32 [512, 4, 4, 512], replicated
- left_env: bfloat16 [128, 512, 512], P('terms')
- two_site: bfloat16 [128, 16, 16], P('terms')
- right_env: bfloat16 [128, 512, 512], P('terms', 'rows')
Outputs:
- output 1: float32 [7, 512, 4, 4, 512], P(None, 'terms', None, None, 'rows')
- output 2: float32 [6], replicated
- output 3: float32 [6], replicated
All inputs are finite; a program needn't handle non-finite values.
Results may differ from a plain program's by a relative error of at most 0.0125741.
Values are sent between devices in bfloat16 or wider.
A program may use at most 1 GiB of HBM per device.

v0:
```python
import jax
import jax.numpy as jnp
from jax import lax
from jax.sharding import PartitionSpec as P

KRYLOV_STEPS = 6


def local_sigma(full_u, left_loc, two_loc, right_loc):
    right_part = jnp.einsum('cpe,kbe->kcpb', full_u, right_loc, preferred_element_type=jnp.float32).astype(jnp.bfloat16)
    mid_part = jnp.einsum('kqp,kcpb->kcqb', two_loc, right_part, preferred_element_type=jnp.float32).astype(jnp.bfloat16)
    return jnp.einsum('kac,kcqb->aqb', left_loc, mid_part, preferred_element_type=jnp.float32)


def solution(mesh):
    terms_count = mesh.shape['terms']
    rows_count = mesh.shape['rows']

    def body_fn(wavefunc, left_loc, two_loc, right_loc):
        bond_dim = wavefunc.shape[0]
        phys_dim = wavefunc.shape[1]
        pair_dim = phys_dim * phys_dim
        elem_count = float(bond_dim * bond_dim * pair_dim)
        row_block = bond_dim // terms_count
        col_block = bond_dim // rows_count
        term_idx = lax.axis_index('terms')
        row_idx = lax.axis_index('rows')
        init_scale = jnp.sqrt(jnp.mean(wavefunc * wavefunc))
        first_vec = (wavefunc / init_scale).reshape(bond_dim, pair_dim, bond_dim)
        cur_vec = lax.dynamic_slice(first_vec, (term_idx * row_block, 0, row_idx * col_block), (row_block, pair_dim, col_block))
        prev_vec = jnp.zeros_like(cur_vec)
        prev_beta = jnp.zeros((), jnp.float32)
        full_u = first_vec.astype(jnp.bfloat16)
        vec_list = [cur_vec]
        alpha_list = []
        beta_list = []
        for step_idx in range(KRYLOV_STEPS):
            part_sigma = local_sigma(full_u, left_loc, two_loc, right_loc)
            w_vec = lax.psum_scatter(part_sigma, 'terms', scatter_dimension=0, tiled=True)
            alpha_val = lax.psum(jnp.sum(w_vec * cur_vec), ('rows', 'terms')) / elem_count
            w_vec = w_vec - alpha_val * cur_vec - prev_beta * prev_vec
            beta_val = jnp.sqrt(lax.psum(jnp.sum(w_vec * w_vec), ('rows', 'terms')) / elem_count)
            next_vec = w_vec / beta_val
            vec_list.append(next_vec)
            alpha_list.append(alpha_val)
            beta_list.append(beta_val)
            prev_vec, cur_vec, prev_beta = cur_vec, next_vec, beta_val
            if step_idx + 1 < KRYLOV_STEPS:
                col_gather = lax.all_gather(next_vec.astype(jnp.bfloat16), 'rows', axis=2, tiled=True)
                full_u = lax.all_gather(col_gather, 'terms', axis=0, tiled=True)
        krylov = jnp.stack(vec_list).reshape(KRYLOV_STEPS + 1, row_block, phys_dim, phys_dim, col_block)
        return krylov, jnp.stack(alpha_list), jnp.stack(beta_list)

    return jax.shard_map(body_fn, mesh=mesh, in_specs=(P(), P('terms'), P('terms'), P('terms', 'rows')), out_specs=(P(None, 'terms', None, None, 'rows'), P(), P()), check_vma=False)
```

profile of v0, /device:TPU:1, one launch (start us, length us, event | category | flops | bytes accessed | tf_op | source)
XLA Modules:
  0.0 1651.8 jit_solution(13343388386890977791)
XLA Ops:
  7.2 1.1 copy.40
  8.3 10.9 multiply_reduce_fusion
  19.9 12.4 broadcast_divide_fusion
  32.3 19.3 %copy.9 = f32[512,4,4,512]{0,3,2,1:T(8,128)} copy(f32[512,4,4,512]{3,2,1,0:T(4,128)} %bitcast.172) | data formatting | bytes 33554432 | tf_op jit(solution)/shard_map/div | solution.py:29
  51.6 14.6 convert_bitcast_fusion.5
  66.2 22.1 %fusion.10 = f32[16,8,512,1]{2,0,1,3:T(8,128)S(1)} fusion(bf16[64,512,512]{2,1,0:T(8,128)(2,1)} %param.5, bf16[64,16,16,1]{2,1,3,0:T(8,128)(2,1)S(1)} %copy.40, bf16[64,512,16,8]{1,3,0,2:T(8,128)(2,1)} %convert_bitcast_fusion.5), kind=kOutput, calls=%fused_computation.10 | convolution fusion | flops 4433379328 | bytes 42237952 | tf_op jit(solution)/shard_map/kac,kcqb->aqb/dot_general | solution.py:12
  88.3 0.9 copy.155
  89.2 14.2 reduce-scatter.7.cloned.1.call-done
  103.4 1.6 multiply_reduce_fusion.12
  105.0 66.5 %psum.84 = f32[]{:T(128)} all-reduce(f32[]{:T(128)} %get-tuple-element.23), channel_id=1, replica_groups=mesh['rows'=64,'terms'=2] {'rows','terms'}, use_global_device_ids=true, to_apply=%region_3.0 | all-reduce | flops 1 | bytes 8 | tf_op jit(solution)/shard_map/psum | solution.py:40
  172.2 1.5 multiply_reduce_fusion.11
  173.8 62.7 %psum.85 = f32[]{:T(128)} all-reduce(f32[]{:T(128)} %multiply_reduce_fusion.11), channel_id=1, replica_groups=mesh['rows'=64,'terms'=2] {'rows','terms'}, use_global_device_ids=true, to_apply=%region_5.0 | all-reduce | flops 1 | bytes 8 | tf_op jit(solution)/shard_map/psum | solution.py:42
  237.1 1.6 fusion.100
  238.8 70.1 %all-gather.11.cloned.1.call-done = bf16[256,16,512]{0,2,1:T(8,128)(2,1)} async-done(((bf16[256,16,8]{0,2,1:T(8,128)(2,1)}), bf16[256,16,512]{0,2,1:T(8,128)(2,1)}) %all-gather.11.cloned.1.call-update) | async-done | bytes 4194320 | tf_op jit(solution)/shard_map/all_gather | solution.py:49
  309.1 26.0 %all-gather.13.cloned.1.call-done = bf16[512,16,512]{0,2,1:T(8,128)(2,1)} async-done(((bf16[256,16,512]{0,2,1:T(8,128)(2,1)}), bf16[512,16,512]{0,2,1:T(8,128)(2,1)}) %all-gather.13.cloned.1.call-update) | async-done | bytes 8388624 | tf_op jit(solution)/shard_map/all_gather | solution.py:50
  335.1 10.4 convert_bitcast_fusion.4
  345.5 27.3 %fusion.8 = f32[16,8,512,1]{2,0,1,3:T(8,128)S(1)} fusion(bf16[64,512,512]{2,1,0:T(8,128)(2,1)} %param.5, bf16[64,16,16,1]{2,1,3,0:T(8,128)(2,1)S(1)} %copy.40, bf16[64,512,16,8]{1,0,3,2:T(8,128)(2,1)} %convert_bitcast_fusion.4), kind=kOutput, calls=%fused_computation.8 | convolution fusion | flops 4433379328 | bytes 42237952 | tf_op jit(solution)/shard_map/kac,kcqb->aqb/dot_general | solution.py:12
  372.8 0.9 copy.154
  373.7 11.9 reduce-scatter.9.cloned.1.call-done
  385.6 1.5 multiply_reduce_fusion.10
  387.2 66.5 %psum.86 = f32[]{:T(128)} all-reduce(f32[]{:T(128)} %multiply_reduce_fusion.10), channel_id=1, replica_groups=mesh['rows'=64,'terms'=2] {'rows','terms'}, use_global_device_ids=true, to_apply=%region_8.0 | all-reduce | flops 1 | bytes 8 | tf_op jit(solution)/shard_map/psum | solution.py:40
  454.3 1.5 multiply_reduce_fusion.9
  455.9 62.7 %psum.87 = f32[]{:T(128)} all-reduce(f32[]{:T(128)} %get-tuple-element.19), channel_id=1, replica_groups=mesh['rows'=64,'terms'=2] {'rows','terms'}, use_global_device_ids=true, to_apply=%region_10.0 | all-reduce | flops 1 | bytes 8 | tf_op jit(solution)/shard_map/psum | solution.py:42
  520.0 70.1 %all-gather.15.cloned.1.call-done = bf16[256,16,512]{0,2,1:T(8,128)(2,1)} async-done(((bf16[256,16,8]{0,2,1:T(8,128)(2,1)}), bf16[256,16,512]{0,2,1:T(8,128)(2,1)}) %all-gather.15.cloned.1.call-update) | async-done | bytes 4194320 | tf_op jit(solution)/shard_map/all_gather | solution.py:49
  590.5 25.6 %all-gather.17.cloned.1.call-done = bf16[512,16,512]{0,2,1:T(8,128)(2,1)} async-done(((bf16[256,16,512]{0,2,1:T(8,128)(2,1)}), bf16[512,16,512]{0,2,1:T(8,128)(2,1)}) %all-gather.17.cloned.1.call-update) | async-done | bytes 8388624 | tf_op jit(solution)/shard_map/all_gather | solution.py:50
  616.2 10.4 convert_bitcast_fusion.3
  626.5 27.3 %fusion.6 = f32[16,8,512,1]{2,0,1,3:T(8,128)S(1)} fusion(bf16[64,512,512]{2,1,0:T(8,128)(2,1)} %param.5, bf16[64,16,16,1]{2,1,3,0:T(8,128)(2,1)S(1)} %copy.40, bf16[64,512,16,8]{1,0,3,2:T(8,128)(2,1)} %convert_bitcast_fusion.3), kind=kOutput, calls=%fused_computation.6 | convolution fusion | flops 4433379328 | bytes 42237952 | tf_op jit(solution)/shard_map/kac,kcqb->aqb/dot_general | solution.py:12
  653.8 0.9 copy.153
  654.8 11.9 reduce-scatter.11.cloned.1.call-done
  666.7 1.5 multiply_reduce_fusion.8
  668.2 66.5 %psum.88 = f32[]{:T(128)} all-reduce(f32[]{:T(128)} %multiply_reduce_fusion.8), channel_id=1, replica_groups=mesh['rows'=64,'terms'=2] {'rows','terms'}, use_global_device_ids=true, to_apply=%region_13.0 | all-reduce | flops 1 | bytes 8 | tf_op jit(solution)/shard_map/psum | solution.py:40
  735.4 1.5 multiply_reduce_fusion.7
  737.0 62.7 %psum.89 = f32[]{:T(128)} all-reduce(f32[]{:T(128)} %get-tuple-element.15), channel_id=1, replica_groups=mesh['rows'=64,'terms'=2] {'rows','terms'}, use_global_device_ids=true, to_apply=%region_15.0 | all-reduce | flops 1 | bytes 8 | tf_op jit(solution)/shard_map/psum | solution.py:42
  801.0 70.1 %all-gather.19.cloned.1.call-done = bf16[256,16,512]{0,2,1:T(8,128)(2,1)} async-done(((bf16[256,16,8]{0,2,1:T(8,128)(2,1)}), bf16[256,16,512]{0,2,1:T(8,128)(2,1)}) %all-gather.19.cloned.1.call-update) | async-done | bytes 4194320 | tf_op jit(solution)/shard_map/all_gather | solution.py:49
  871.4 26.0 %all-gather.21.cloned.1.call-done = bf16[512,16,512]{0,2,1:T(8,128)(2,1)} async-done(((bf16[256,16,512]{0,2,1:T(8,128)(2,1)}), bf16[512,16,512]{0,2,1:T(8,128)(2,1)}) %all-gather.21.cloned.1.call-update) | async-done | bytes 8388624 | tf_op jit(solution)/shard_map/all_gather | solution.py:50
  897.4 10.4 convert_bitcast_fusion.2
  907.8 27.3 %fusion.4 = f32[16,8,512,1]{2,0,1,3:T(8,128)S(1)} fusion(bf16[64,512,512]{2,1,0:T(8,128)(2,1)} %param.5, bf16[64,16,16,1]{2,1,3,0:T(8,128)(2,1)S(1)} %copy.40, bf16[64,512,16,8]{1,0,3,2:T(8,128)(2,1)} %convert_bitcast_fusion.2), kind=kOutput, calls=%fused_computation.4 | convolution fusion | flops 4433379328 | bytes 42237952 | tf_op jit(solution)/shard_map/kac,kcqb->aqb/dot_general | solution.py:12
  935.1 0.9 copy.152
  936.0 11.9 reduce-scatter.13.cloned.1.call-done
  947.9 1.5 multiply_reduce_fusion.6
  949.5 66.5 %psum.90 = f32[]{:T(128)} all-reduce(f32[]{:T(128)} %multiply_reduce_fusion.6), channel_id=1, replica_groups=mesh['rows'=64,'terms'=2] {'rows','terms'}, use_global_device_ids=true, to_apply=%region_18.0 | all-reduce | flops 1 | bytes 8 | tf_op jit(solution)/shard_map/psum | solution.py:40
  1016.6 1.5 multiply_reduce_fusion.5
  1018.2 62.6 %psum.91 = f32[]{:T(128)} all-reduce(f32[]{:T(128)} %get-tuple-element.11), channel_id=1, replica_groups=mesh['rows'=64,'terms'=2] {'rows','terms'}, use_global_device_ids=true, to_apply=%region_20.0 | all-reduce | flops 1 | bytes 8 | tf_op jit(solution)/shard_map/psum | solution.py:42
  1082.2 69.9 %all-gather.23.cloned.1.call-done = bf16[256,16,512]{0,2,1:T(8,128)(2,1)} async-done(((bf16[256,16,8]{0,2,1:T(8,128)(2,1)}), bf16[256,16,512]{0,2,1:T(8,128)(2,1)}) %all-gather.23.cloned.1.call-update) | async-done | bytes 4194320 | tf_op jit(solution)/shard_map/all_gather | solution.py:49
  1152.4 25.8 %all-gather.25.cloned.1.call-done = bf16[512,16,512]{0,2,1:T(8,128)(2,1)} async-done(((bf16[256,16,512]{0,2,1:T(8,128)(2,1)}), bf16[512,16,512]{0,2,1:T(8,128)(2,1)}) %all-gather.25.cloned.1.call-update) | async-done | bytes 8388624 | tf_op jit(solution)/shard_map/all_gather | solution.py:50
  1178.2 10.4 convert_bitcast_fusion.1
  1188.6 27.3 %fusion.2 = f32[16,8,512,1]{2,0,1,3:T(8,128)S(1)} fusion(bf16[64,512,512]{2,1,0:T(8,128)(2,1)} %param.5, bf16[64,16,16,1]{2,1,3,0:T(8,128)(2,1)S(1)} %copy.40, bf16[64,512,16,8]{1,0,3,2:T(8,128)(2,1)} %convert_bitcast_fusion.1), kind=kOutput, calls=%fused_computation.2 | convolution fusion | flops 4433379328 | bytes 42237952 | tf_op jit(solution)/shard_map/kac,kcqb->aqb/dot_general | solution.py:12
  1215.9 0.9 copy.151
  1216.8 11.9 reduce-scatter.15.cloned.1.call-done
  1228.7 1.5 multiply_reduce_fusion.4
  1230.3 66.5 %psum.92 = f32[]{:T(128)} all-reduce(f32[]{:T(128)} %multiply_reduce_fusion.4), channel_id=1, replica_groups=mesh['rows'=64,'terms'=2] {'rows','terms'}, use_global_device_ids=true, to_apply=%region_23.0 | all-reduce | flops 1 | bytes 8 | tf_op jit(solution)/shard_map/psum | solution.py:40
  1297.4 1.5 multiply_reduce_fusion.3
  1299.0 62.7 %psum.93 = f32[]{:T(128)} all-reduce(f32[]{:T(128)} %get-tuple-element.7), channel_id=1, replica_groups=mesh['rows'=64,'terms'=2] {'rows','terms'}, use_global_device_ids=true, to_apply=%region_25.0 | all-reduce | flops 1 | bytes 8 | tf_op jit(solution)/shard_map/psum | solution.py:42
  1363.1 70.1 %all-gather.27.cloned.1.call-done = bf16[256,16,512]{0,2,1:T(8,128)(2,1)} async-done(((bf16[256,16,8]{0,2,1:T(8,128)(2,1)}), bf16[256,16,512]{0,2,1:T(8,128)(2,1)}) %all-gather.27.cloned.1.call-update) | async-done | bytes 4194320 | tf_op jit(solution)/shard_map/all_gather | solution.py:49
  1433.5 25.8 %all-gather.29.cloned.1.call-done = bf16[512,16,512]{0,2,1:T(8,128)(2,1)} async-done(((bf16[256,16,512]{0,2,1:T(8,128)(2,1)}), bf16[512,16,512]{0,2,1:T(8,128)(2,1)}) %all-gather.29.cloned.1.call-update) | async-done | bytes 8388624 | tf_op jit(solution)/shard_map/all_gather | solution.py:50
  1459.3 10.4 convert_bitcast_fusion
  1469.6 27.3 %fusion = f32[16,8,512,1]{2,0,1,3:T(8,128)S(1)} fusion(bf16[64,512,512]{2,1,0:T(8,128)(2,1)} %param.5, bf16[64,16,16,1]{2,1,3,0:T(8,128)(2,1)S(1)} %copy.40, bf16[64,512,16,8]{1,0,3,2:T(8,128)(2,1)} %convert_bitcast_fusion), kind=kOutput, calls=%fused_computation | convolution fusion | flops 4433379328 | bytes 42237952 | tf_op jit(solution)/shard_map/kac,kcqb->aqb/dot_general | solution.py:12
  1496.9 0.9 copy.150
  1497.9 11.9 reduce-scatter.17.cloned.1.call-done
  1509.8 1.5 multiply_reduce_fusion.2
  1511.4 66.6 %psum.94 = f32[]{:T(128)} all-reduce(f32[]{:T(128)} %multiply_reduce_fusion.2), channel_id=1, replica_groups=mesh['rows'=64,'terms'=2] {'rows','terms'}, use_global_device_ids=true, to_apply=%region_28.0 | all-reduce | flops 1 | bytes 8 | tf_op jit(solution)/shard_map/psum | solution.py:40
  1578.6 1.5 multiply_reduce_fusion.1
  1580.1 62.6 %psum.95 = f32[]{:T(128)} all-reduce(f32[]{:T(128)} %get-tuple-element.3), channel_id=1, replica_groups=mesh['rows'=64,'terms'=2] {'rows','terms'}, use_global_device_ids=true, to_apply=%region_30.0 | all-reduce | flops 1 | bytes 8 | tf_op jit(solution)/shard_map/psum | solution.py:42
  1643.5 0.7 stack.80
  (49 shorter events, 5.5 us)
Async XLA Ops:
  7.2 96.3 %reduce-scatter.7.cloned.1.call-start = ((), (), s32[]{:S(2)}) async-start(), calls=%async_computation.6 | async-start | bytes 393216 | tf_op jit(solution)/shard_map/reduce_scatter | solution.py:39
  32.3 19.3 %copy-start = (bf16[64,8,512]{2,1,0:T(8,128)(2,1)S(1)}, bf16[64,8,512]{2,1,0:T(8,128)(2,1)}, u32[]{:S(2)}) copy-start(bf16[64,8,512]{2,1,0:T(8,128)(2,1)} %param.7) | copy-start | bytes 1572868
  89.2 219.6 %all-gather.11.cloned.1.call-start = ((), (), s32[]{:S(2)}) async-start(), calls=%async_computation.7 | async-start | bytes 4259840 | tf_op jit(solution)/shard_map/all_gather | solution.py:49
  238.7 96.4 %all-gather.13.cloned.1.call-start = ((), (), s32[]{:S(2)}) async-start(), calls=%async_computation.8 | async-start | bytes 12582912 | tf_op jit(solution)/shard_map/all_gather | solution.py:50
  308.9 76.8 %reduce-scatter.9.cloned.1.call-start = ((), (), s32[]{:S(2)}) async-start(), calls=%async_computation.9 | async-start | bytes 393216 | tf_op jit(solution)/shard_map/reduce_scatter | solution.py:39
  373.6 216.4 %all-gather.15.cloned.1.call-start = ((), (), s32[]{:S(2)}) async-start(), calls=%async_computation.10 | async-start | bytes 4259840 | tf_op jit(solution)/shard_map/all_gather | solution.py:49
  519.9 96.2 %all-gather.17.cloned.1.call-start = ((), (), s32[]{:S(2)}) async-start(), calls=%async_computation.11 | async-start | bytes 12582912 | tf_op jit(solution)/shard_map/all_gather | solution.py:50
  590.1 76.6 %reduce-scatter.11.cloned.1.call-start = ((), (), s32[]{:S(2)}) async-start(), calls=%async_computation.12 | async-start | bytes 393216 | tf_op jit(solution)/shard_map/reduce_scatter | solution.py:39
  654.7 216.4 %all-gather.19.cloned.1.call-start = ((), (), s32[]{:S(2)}) async-start(), calls=%async_computation.13 | async-start | bytes 4259840 | tf_op jit(solution)/shard_map/all_gather | solution.py:49
  801.0 96.4 %all-gather.21.cloned.1.call-start = ((), (), s32[]{:S(2)}) async-start(), calls=%async_computation.14 | async-start | bytes 12582912 | tf_op jit(solution)/shard_map/all_gather | solution.py:50
  871.2 76.8 %reduce-scatter.13.cloned.1.call-start = ((), (), s32[]{:S(2)}) async-start(), calls=%async_computation.15 | async-start | bytes 393216 | tf_op jit(solution)/shard_map/reduce_scatter | solution.py:39
  935.9 216.2 %all-gather.23.cloned.1.call-start = ((), (), s32[]{:S(2)}) async-start(), calls=%async_computation.16 | async-start | bytes 4259840 | tf_op jit(solution)/shard_map/all_gather | solution.py:49
  1082.2 96.0 %all-gather.25.cloned.1.call-start = ((), (), s32[]{:S(2)}) async-start(), calls=%async_computation.17 | async-start | bytes 12582912 | tf_op jit(solution)/shard_map/all_gather | solution.py:50
  1152.1 76.6 %reduce-scatter.15.cloned.1.call-start = ((), (), s32[]{:S(2)}) async-start(), calls=%async_computation.18 | async-start | bytes 393216 | tf_op jit(solution)/shard_map/reduce_scatter | solution.py:39
  1216.8 216.4 %all-gather.27.cloned.1.call-start = ((), (), s32[]{:S(2)}) async-start(), calls=%async_computation.19 | async-start | bytes 4259840 | tf_op jit(solution)/shard_map/all_gather | solution.py:49
  1363.0 96.2 %all-gather.29.cloned.1.call-start = ((), (), s32[]{:S(2)}) async-start(), calls=%async_computation.20 | async-start | bytes 12582912 | tf_op jit(solution)/shard_map/all_gather | solution.py:50
  1433.2 76.6 %reduce-scatter.17.cloned.1.call-start = ((), (), s32[]{:S(2)}) async-start(), calls=%async_computation.21 | async-start | bytes 393216 | tf_op jit(solution)/shard_map/reduce_scatter | solution.py:39
  1643.5 1.3 copy-start.1
Sparse Core Ops, SparseCore 0:
  89.3 14.0 reduce-scatter.6
  238.8 69.9 all-gather.10
  310.5 24.5 all-gather.12
  373.8 11.8 reduce-scatter.8
  520.0 69.9 all-gather.14
  591.6 24.5 all-gather.16
  654.8 11.8 reduce-scatter.10
  801.1 69.9 all-gather.18
  872.8 24.5 all-gather.20
  936.1 11.8 reduce-scatter.12
  1082.3 69.7 all-gather.22
  1153.6 24.5 all-gather.24
  1216.9 11.8 reduce-scatter.14
  1363.2 69.9 all-gather.26
  1434.7 24.5 all-gather.28
  1497.9 11.8 reduce-scatter.16
where the time goes:
time: 1660 us; the launch traced here: 1650 us
  blocking collectives  775 us (47%)
  waiting for transfers between devices  553 us (33%)
  matrix products  225 us (14%)
  other arithmetic  46.1 us (3%)
  local copies, waits for them, and re-layouts  26.9 us (2%)
  between operations  23.3 us (1%)
    psum x6, blocking collectives, body_fn(): lax.psum(jnp.sum(w_vec * cur_vec), ('rows', 'terms')) / elem_count  399 us
    psum x6, blocking collectives, body_fn(): lax.psum(jnp.sum(w_vec * w_vec), ('rows', 'terms')) / elem_count  376 us
    all_gather x5, waiting for transfers between devices, body_fn(): lax.all_gather(next_vec.astype(jnp.bfloat16), 'rows', axis=2, tiled=True)  350 us
    dot_general x6, matrix products, local_sigma(): jnp.einsum('kac,kcqb->aqb', left_loc, mid_part, preferred_element_type=jn...  159 us
    all_gather x5, waiting for transfers between devices, body_fn(): full_u = lax.all_gather(col_gather, 'terms', axis=0, tiled=True)  129 us
    reduce_scatter x6, waiting for transfers between devices, body_fn(): lax.psum_scatter(part_sigma, 'terms', scatter_dimension=0, tiled=True)  73.8 us
    dot_general x6, matrix products, local_sigma(): jnp.einsum('cpe,kbe->kcpb', full_u, right_loc, preferred_element_type=jnp...  66.4 us
  transfers between devices with their start and end apart: 16, of which 16 were waited for; matrix products, arithmetic and copies ran while one was open for 0% of the time, Pallas kernels for 0%

commit v1 on v0

v1 whole, which is shorter than its diff:
```python
import jax
import jax.numpy as jnp
from jax import lax
from jax.experimental import pallas as pl
from jax.experimental.pallas import tpu as pltpu
from jax.sharding import PartitionSpec as P

STEPS = 6
F32 = jnp.float32
BF16 = jnp.bfloat16
MESH = pl.DeviceIdType.MESH
NT = 64


def total(x):
    return jnp.sum(jnp.sum(x, axis=1, keepdims=True), axis=0, keepdims=True)


def col_sum(x):
    return jnp.sum(x, axis=0, keepdims=True)


def kernel(elem_count, u0_ref, v0_ref, kr0_ref, left_ref, right_ref, two_ref, kr_ref, ab_ref,
           u_ref, rin, rb, lb, wt, y_ref, z_ref, acc_o, acc_m, recv_s, recv_x, vecs, kbuf, red_a, red_b,
           ld_sem, r_send, r_recv, s_send, s_recv, x_send, x_recv, a_send, a_recv, b_send, b_recv,
           g1_send, g1_recv, g2_send, g2_recv, g3_send, g3_recv, k_send, k_recv):
    r = lax.axis_index('rows')
    c = lax.axis_index('terms')
    x = lax.rem(r, 4)
    y = lax.rem(r // 4, 4)
    z = r // 16
    row_base = r - x

    def rcopy(src, dst, ssem, rsem, row, core):
        return pltpu.make_async_remote_copy(src_ref=src, dst_ref=dst, send_sem=ssem, recv_sem=rsem,
                                            device_id=(row, core), device_id_type=MESH)

    cp_l = pltpu.make_async_copy(left_ref.at[:, pl.ds(pl.multiple_of(x * 128, 128), 128), :], lb, ld_sem.at[0])
    cp_u = pltpu.make_async_copy(u0_ref, u_ref, ld_sem.at[1])
    cp_r = pltpu.make_async_copy(right_ref, rin.at[x], ld_sem.at[2])
    cp_r.start()
    cp_u.start()
    cp_l.start()
    cp_r.wait()
    r_copies = []
    for d in range(1, 4):
        px = lax.rem(x + d, 4)
        cp = rcopy(rin.at[x], rin.at[x], r_send.at[d - 1], r_recv.at[d - 1], row_base + px, c)
        cp.start()
        r_copies.append(cp)

    lane16 = lax.broadcasted_iota(jnp.int32, (16, 256), 1)
    row16 = lax.broadcasted_iota(jnp.int32, (16, 256), 0)
    e_col = (lane16 // 16 == row16).astype(BF16)
    row_e = lax.broadcasted_iota(jnp.int32, (256, 16), 0)
    lane_e = lax.broadcasted_iota(jnp.int32, (256, 16), 1)
    e_row = (row_e // 16 == lane_e).astype(BF16)
    row_m = lax.broadcasted_iota(jnp.int32, (256, 256), 0)
    lane_m = lax.broadcasted_iota(jnp.int32, (256, 256), 1)
    diag = lax.rem(row_m, 16) == lax.rem(lane_m, 16)

    def build_w(k, carry):
        wk = two_ref[pl.ds(pl.multiple_of(k * 16, 16), 16), :]
        wide = jnp.dot(wk, e_col, preferred_element_type=F32).astype(BF16)
        full = jnp.dot(e_row, wide, preferred_element_type=F32)
        wt[k] = jnp.where(diag, full, 0.0).astype(BF16)
        return carry

    lax.fori_loop(0, NT, build_w, 0)

    vecs[0] = v0_ref[...]
    kbuf[0] = kr0_ref[...]
    for cp in r_copies:
        cp.wait()

    def build_r(i, carry):
        rows = pl.ds(pl.multiple_of(i * 64, 64), 64)
        for bhi in range(2):
            lo = rin[2 * bhi, rows, :].astype(F32).reshape(8, 8, 512)
            hi = rin[2 * bhi + 1, rows, :].astype(F32).reshape(8, 8, 512)
            both = jnp.concatenate([lo, hi], axis=1).reshape(128, 512)
            rb[bhi, pl.ds(pl.multiple_of(i * 128, 128), 128), :] = both.astype(BF16)
        return carry

    lax.fori_loop(0, 8, build_r, 0)
    cp_u.wait()
    cp_l.wait()

    row_id = lax.broadcasted_iota(jnp.int32, (8, 128), 0)
    ab_ref[...] = jnp.zeros_like(ab_ref)

    def pack(p, n, am, rr, ss):
        out = jnp.where(row_id == 0, p, 0.0)
        out = jnp.where(row_id == 1, n, out)
        out = jnp.where(row_id == 2, am, out)
        out = jnp.where(row_id == 3, rr, out)
        return jnp.where(row_id == 4, ss, out)

    def safe_div(num, den):
        ok = den > 0.0
        return jnp.where(ok, num / jnp.where(ok, den, 1.0), 0.0)

    def merge(p, n, am, rr, ss):
        n_all = col_sum(n)
        mean = safe_div(col_sum(am * n), n_all)
        gap = mean - am
        r_all = col_sum(rr + gap * (gap * n - 2.0 * ss))
        return col_sum(p), n_all, mean, r_all, col_sum(ss)

    def step(j, prev_beta):
        def s1(pp, carry):
            w = jnp.concatenate([u_ref[2 * pp].reshape(512, 128), u_ref[2 * pp + 1].reshape(512, 128)], axis=1)
            for bhi in range(2):
                for mc in range(2):
                    o = jnp.dot(rb[bhi, mc * 512:(mc + 1) * 512, :], w, preferred_element_type=F32)
                    o = o.astype(BF16).reshape(32, 16, 256)
                    y_ref[mc * 32:(mc + 1) * 32, bhi, 2 * pp] = o[:, :, :128]
                    y_ref[mc * 32:(mc + 1) * 32, bhi, 2 * pp + 1] = o[:, :, 128:]
            return carry

        lax.fori_loop(0, 8, s1, 0)

        def s2(kk, carry):
            for i in range(4):
                k = kk * 4 + i
                rhs = jnp.concatenate([y_ref[k, 0].reshape(256, 128), y_ref[k, 1].reshape(256, 128)], axis=1)
                o = jnp.dot(wt[k], rhs, preferred_element_type=F32).astype(BF16)
                z_ref[0, k] = o[:, :128]
                z_ref[1, k] = o[:, 128:]
            return carry

        lax.fori_loop(0, NT // 4, s2, 0)

        def s3(bhi, acc):
            def part(kc):
                lhs = jnp.concatenate([z_ref[bhi, kc * 8 + i] for i in range(8)], axis=1)
                rhs = lb[pl.ds(kc * 8, 8)].reshape(1024, 512)
                return jnp.dot(lhs, rhs, preferred_element_type=F32)

            o = part(0)
            for i in range(4):
                acc[i] = o[:, i * 128:(i + 1) * 128]

            def more(kc, carry):
                o = part(kc)
                for i in range(4):
                    acc[i] += o[:, i * 128:(i + 1) * 128]
                return carry

            lax.fori_loop(1, 8, more, 0)

        s3(1 - c, acc_o)
        cp_s = rcopy(acc_o, recv_s, s_send.at[0], s_recv.at[0], r, 1 - c)
        cp_s.start()
        s3(c, acc_m)
        cp_s.wait()
        for i in range(4):
            acc_m[i] += recv_s[i]
        x_copies = []
        for d in range(1, 4):
            px = lax.rem(x + d, 4)
            cp = rcopy(acc_m.at[px], recv_x.at[d - 1], x_send.at[d - 1], x_recv.at[d - 1], row_base + px, c)
            cp.start()
            x_copies.append(cp)
        for cp in x_copies:
            cp.wait()
        w_vec = (acc_m[x] + recv_x[0]) + (recv_x[1] + recv_x[2])
        v_cur = vecs[j]
        v_old = vecs[lax.max(j - 1, 0)]

        w_res = w_vec - prev_beta * v_old
        n_loc = total(v_cur * v_cur)
        a_loc = safe_div(total(w_res * v_cur), n_loc)
        e_loc = w_res - a_loc * v_cur
        red_a[0] = pack(total(w_vec * v_cur), n_loc, a_loc, total(e_loc * e_loc), total(e_loc * v_cur))

        a_copies = []
        for d in range(1, 8):
            slot = lax.rem(x * 2 + c + d, 8)
            cp = rcopy(red_a.at[0], red_a.at[d], a_send.at[d - 1], a_recv.at[d - 1], row_base + slot // 2, lax.rem(slot, 2))
            cp.start()
            a_copies.append(cp)
        for cp in a_copies:
            cp.wait()
        me = x * 2 + c
        blocks = [red_a[lax.rem(me - s + 8, 8)] for s in range(8)]

        def gather_rows(blks, i):
            return jnp.concatenate([bk[i:i + 1, :] for bk in blks], axis=0)

        red_b[0] = pack(*merge(*[gather_rows(blocks, i) for i in range(5)]))
        b_copies = []
        g = z * 4 + y
        for d in range(1, 16):
            pg = lax.rem(g + d, 16)
            cp = rcopy(red_b.at[0], red_b.at[d], b_send.at[d - 1], b_recv.at[d - 1], pg * 4 + x, c)
            cp.start()
            b_copies.append(cp)
        for cp in b_copies:
            cp.wait()
        blocks = [red_b[lax.rem(g - s + 16, 16)] for s in range(16)]
        p_all, n_all, a_all, r_all, s_all = [gather_rows(blocks, i) for i in range(5)]
        alpha = col_sum(p_all) / elem_count
        gap = alpha - a_all
        beta = jnp.sqrt(col_sum(r_all + gap * (gap * n_all - 2.0 * s_all)) / elem_count)
        alpha_s = alpha[:, :1]
        beta_s = beta[:, :1]

        v_new = (w_vec - alpha_s * v_cur - prev_beta * v_old) / beta_s
        vecs[j + 1] = v_new
        ab_ref[pl.ds(j, 1), :] = alpha
        ab_ref[pl.ds(8 + j, 1), :] = beta

        for h in range(2):
            dst_x = 2 * c + h
            dst_c = x // 2
            is_me = jnp.logical_and(dst_x == x, dst_c == c)
            lanes = pl.ds(pl.multiple_of(lax.rem(x, 2) * 128, 128), 128)
            src = vecs.at[j + 1].reshape(16, 16, 128).at[:, h * 8:(h + 1) * 8, :]

            @pl.when(jnp.logical_not(is_me))
            def _():
                rcopy(src, kbuf.at[j + 1, :, :, lanes], k_send.at[j, h], k_recv.at[j, lax.rem(x, 2)],
                      row_base + dst_x, dst_c).start()

            @pl.when(is_me)
            def _():
                kbuf[j + 1, :, :, lanes] = v_new.reshape(16, 16, 128)[:, h * 8:(h + 1) * 8, :]

        @pl.when(j < STEPS - 1)
        def _():
            u_ref[:, z, y, c] = v_new.astype(BF16).reshape(16, 16, 128)
            lo, hi = pl.ds(0, 8), pl.ds(8, 8)
            cps = []
            for d in range(1, 4):
                zrow = lax.rem(z + d, 4) * 16 + y * 4 + x
                yrow = z * 16 + lax.rem(y + d, 4) * 4 + x
                s1_ = u_ref.at[lo, z, y, c]
                s2_ = u_ref.at[hi, z, y, c]
                cps.append(rcopy(s1_, s1_, g1_send.at[0, d - 1], g1_recv.at[0, d - 1], zrow, c))
                cps.append(rcopy(s2_, s2_, g1_send.at[1, d - 1], g1_recv.at[1, d - 1], yrow, c))
            for cp in cps:
                cp.start()
            for cp in cps:
                cp.wait()
            cps = []
            for d in range(1, 4):
                zrow = lax.rem(z + d, 4) * 16 + y * 4 + x
                yrow = z * 16 + lax.rem(y + d, 4) * 4 + x
                s1_ = u_ref.at[lo, :, y, c]
                s2_ = u_ref.at[hi, z, :, c]
                cps.append(rcopy(s1_, s1_, g2_send.at[0, d - 1], g2_recv.at[0, d - 1], yrow, c))
                cps.append(rcopy(s2_, s2_, g2_send.at[1, d - 1], g2_recv.at[1, d - 1], zrow, c))
            for cp in cps:
                cp.start()
            for cp in cps:
                cp.wait()
            s3_ = u_ref.at[:, :, :, c]
            cp3 = rcopy(s3_, s3_, g3_send.at[0], g3_recv.at[0], r, 1 - c)
            cp3.start()
            cp3.wait()

        return beta_s

    lax.fori_loop(0, STEPS, step, jnp.zeros((1, 1), F32))

    def drain(j, carry):
        for h in range(2):
            dst_x = 2 * c + h
            dst_c = x // 2
            src = vecs.at[j + 1].reshape(16, 16, 128).at[:, h * 8:(h + 1) * 8, :]

            @pl.when(jnp.logical_not(jnp.logical_and(dst_x == x, dst_c == c)))
            def _():
                rcopy(src, kbuf.at[j + 1, :, :, 0:128], k_send.at[j, h], k_recv.at[j, 0],
                      row_base + dst_x, dst_c).wait_send()

        for m in range(2):
            src_x = 2 * c + m
            src_c = x // 2

            @pl.when(jnp.logical_not(jnp.logical_and(src_x == x, src_c == c)))
            def _():
                rcopy(vecs.at[j + 1].reshape(16, 16, 128).at[:, 0:8, :], kbuf.at[j + 1, :, :, m * 128:(m + 1) * 128],
                      k_send.at[j, 0], k_recv.at[j, m], row_base + src_x, src_c).wait_recv()

        return carry

    lax.fori_loop(0, STEPS, drain, 0)
    cp_k = pltpu.make_async_copy(kbuf, kr_ref, ld_sem.at[0])
    cp_k.start()
    cp_k.wait()


def solution(mesh):
    assert mesh.shape['terms'] == 2 and mesh.shape['rows'] == 64

    def body_fn(wavefunc, left_loc, two_loc, right_loc):
        elem_count = float(wavefunc.size)
        row = lax.axis_index('rows')
        core = lax.axis_index('terms')
        xi = lax.rem(row, 4)
        gi = row // 4
        wave = wavefunc.reshape(512, 16, 512)
        scale = jnp.sqrt(jnp.mean(wave * wave))
        slab = lax.dynamic_slice(wave, (xi * 128, 0, 0), (128, 16, 512)) / scale
        u0 = jnp.transpose(slab.astype(BF16), (1, 2, 0)).reshape(16, 4, 4, 2, 16, 128)
        mine = lax.dynamic_slice(slab, (0, 0, gi * 32 + core * 16), (128, 16, 16))
        v0 = jnp.transpose(mine, (1, 2, 0)).reshape(256, 128)
        out0 = lax.dynamic_slice(wave, (core * 256, 0, row * 8), (256, 16, 8)) / scale
        kr0 = jnp.transpose(out0, (1, 2, 0))
        vm = pl.BlockSpec(memory_space=pltpu.VMEM)
        hbm = pl.BlockSpec(memory_space=pl.ANY)
        dma = pltpu.SemaphoreType.DMA
        kr, ab = pl.pallas_call(
            lambda *refs: kernel(elem_count, *refs),
            out_shape=(jax.ShapeDtypeStruct((STEPS + 1, 16, 8, 256), F32), jax.ShapeDtypeStruct((16, 128), F32)),
            in_specs=[hbm, vm, vm, hbm, hbm, vm],
            out_specs=(hbm, vm),
            scratch_shapes=[
                pltpu.VMEM((16, 4, 4, 2, 16, 128), BF16),
                pltpu.VMEM((4, 512, 512), BF16),
                pltpu.VMEM((2, 1024, 512), BF16),
                pltpu.VMEM((NT, 128, 512), BF16),
                pltpu.VMEM((NT, 256, 256), BF16),
                pltpu.VMEM((NT, 2, 16, 16, 128), BF16),
                pltpu.VMEM((2, NT, 256, 128), BF16),
                pltpu.VMEM((4, 256, 128), F32),
                pltpu.VMEM((4, 256, 128), F32),
                pltpu.VMEM((4, 256, 128), F32),
                pltpu.VMEM((3, 256, 128), F32),
                pltpu.VMEM((STEPS + 1, 256, 128), F32),
                pltpu.VMEM((STEPS + 1, 16, 8, 256), F32),
                pltpu.VMEM((8, 8, 128), F32),
                pltpu.VMEM((16, 8, 128), F32),
                dma((3,)), dma((3,)), dma((3,)), dma((1,)), dma((1,)), dma((3,)), dma((3,)),
                dma((7,)), dma((7,)), dma((15,)), dma((15,)),
                dma((2, 3)), dma((2, 3)), dma((2, 3)), dma((2, 3)), dma((1,)), dma((1,)),
                dma((STEPS, 2)), dma((STEPS, 2)),
            ],
            compiler_params=pltpu.CompilerParams(has_side_effects=True, vmem_limit_bytes=60 * 1024 * 1024),
        )(u0, v0, kr0, left_loc, right_loc.reshape(512, 512), two_loc.reshape(1024, 16))
        krylov = jnp.transpose(kr.reshape(STEPS + 1, 4, 4, 8, 256), (0, 4, 1, 2, 3))
        return krylov, ab[:STEPS, 0], ab[8:8 + STEPS, 0]

    return jax.shard_map(body_fn, mesh=mesh, in_specs=(P(), P('terms'), P('terms'), P('terms', 'rows')),
                         out_specs=(P(None, 'terms', None, None, 'rows'), P(), P()), check_vma=False)
```

time: 1660 us -> 370 us (0.22)
  blocking collectives: 775 us -> 0 us
  waiting for transfers between devices: 553 us -> 0 us
  Pallas kernels: 0 us -> 324 us
  matrix products: 225 us -> 0 us
  other arithmetic: 46.1 us -> 18.1 us
  between operations: 23.3 us -> 1.34 us
    psum x12 -> x0, blocking collectives: 775 us -> none  [the longest x6 399 us: body_fn(): lax.psum(jnp.sum(w_vec * cur_vec), ('rows', 'terms')) / elem_count]
    all_gather x10 -> x0, waiting for transfers between devices: 479 us -> none  [the longest x5 350 us: body_fn(): lax.all_gather(next_vec.astype(jnp.bfloat16), 'rows', axis=2, tiled=True)]
    pallas_call x0 -> x1, Pallas kernels: none -> 324 us  [body_fn(): pl.pallas_call(lambda *refs: kernel(elem_count, *refs), out_shape=(jax.Sh...]
    dot_general x12 -> x0, matrix products: 225 us -> none  [the longest x6 159 us: local_sigma(): jnp.einsum('kac,kcqb->aqb', left_loc, mid_part, preferred_element_type=jn...]
    reduce_scatter x6 -> x0, waiting for transfers between devices: 73.8 us -> none  [body_fn(): lax.psum_scatter(part_sigma, 'terms', scatter_dimension=0, tiled=True)]
    unnamed x11 -> x5, local copies, waits for them, and re-layouts: 1.16 us -> 22.4 us
    div x1 -> x0, local copies, waits for them, and re-layouts: 19.3 us -> none  [body_fn(): first_vec = (wavefunc / init_scale).reshape(bond_dim, pair_dim, bond_dim)]
    reduce_sum x13 -> x1, other arithmetic: 29.5 us -> 10.9 us  [body_fn(): scale = jnp.sqrt(jnp.mean(wave * wave))]
  transfers between devices with their start and end apart: 16 -> 0, of which waited for: 16 -> 0; matrix products, arithmetic and copies ran while one was open for 0% -> 0% of each run, Pallas kernels for 0% -> 0%
where the time goes in v1:
time: 370 us; the launch traced here: 369 us
  Pallas kernels  324 us (88%)
  local copies, waits for them, and re-layouts  25.3 us (7%)
  other arithmetic  18.1 us (5%)
    pallas_call x1, Pallas kernels, body_fn(): pl.pallas_call(lambda *refs: kernel(elem_count, *refs), out_shape=(jax.Sh...  324 us
    unnamed x5, local copies, waits for them, and re-layouts  22.4 us
    reduce_sum x1, other arithmetic, body_fn(): scale = jnp.sqrt(jnp.mean(wave * wave))  10.9 us

profile of v1, /device:TPU:1, one launch (start us, length us, event | category | flops | bytes accessed | tf_op | source)
XLA Modules:
  0.0 369.2 jit_solution(7855080043592619904)
XLA Ops:
  0.6 10.9 %multiply_reduce_fusion = f32[]{:T(128)} fusion(f32[512,4,4,512]{3,2,1,0:T(4,128)} %param.4), kind=kLoop, calls=%fused_computation | loop fusion | flops 8388607 | bytes 16777220 | tf_op jit(solution)/shard_map/reduce_sum | solution.py:305
  12.2 0.0 copy-start
  12.2 19.3 %copy.9 = f32[512,4,4,512]{0,3,2,1:T(8,128)} copy(f32[512,4,4,512]{3,2,1,0:T(4,128)} %param.4) | data formatting | bytes 33554432 | tf_op args[0]
  31.5 5.6 %fusion = (bf16[128,16,512]{0,2,1:T(8,128)(2,1)}, f32[128,16,512]{0,2,1:T(8,128)}) fusion(f32[]{:T(128)S(6)} %sqrt.3, f32[512,16,512]{0,2,1:T(8,128)} %bitcast.14, s32[]{:T(128)S(6)} %select_n.17), kind=kLoop, calls=%fused_computation.6 | loop fusion | flops 2097152 | bytes 10485768 | tf_op jit(solution)/shard_map/convert_element_type | solution.py:307
  37.1 1.6 constant_dynamic-slice_fusion
  38.7 1.6 divide_bitcast_fusion.refs_2_
  40.2 0.0 copy-done
  40.2 0.9 copy.10
  41.2 324.5 %shard_map.67 = (f32[7,16,8,256]{3,2,1,0:T(8,128)}, f32[16,128]{1,0:T(8,128)}) custom-call(bf16[16,4,4,2,16,128]{5,4,3,2,1,0:T(8,128)(2,1)} %bitcast.16, f32[256,128]{1,0:T(8,128)} %bitcast.20, f32[16,8,256]{2,1,0:T(8,128)} %divide_bitcast_fusion.refs_2_, bf16[64,512,512]{2,1,0:T(8,128)(2,1)} %refs_3_.1, bf16[512,512]{1,0:T(8,128)(2,1)} %bitcast.19, ...), custom_call_target="tpu_custom_call" | custom-call | tf_op jit(solution)/shard_map/pallas_call | solution.py:315
  365.7 1.3 slice_reduce_fusion
  367.0 2.2 copy.12
Async XLA Ops:
  12.2 28.0 %copy-start = (bf16[64,16,16]{0,2,1:T(8,128)(2,1)S(1)}, bf16[64,16,16]{0,2,1:T(8,128)(2,1)}, u32[]{:S(2)}) copy-start(bf16[64,16,16]{0,2,1:T(8,128)(2,1)} %param.6) | copy-start | bytes 98308

commit v2 on v1

--- a/solution.py
+++ b/solution.py
@@ -20,34 +20,77 @@
     return jnp.sum(x, axis=0, keepdims=True)
 
 
-def kernel(elem_count, u0_ref, v0_ref, kr0_ref, left_ref, right_ref, two_ref, kr_ref, ab_ref,
-           u_ref, rin, rb, lb, wt, y_ref, z_ref, acc_o, acc_m, recv_s, recv_x, vecs, kbuf, red_a, red_b,
-           ld_sem, r_send, r_recv, s_send, s_recv, x_send, x_recv, a_send, a_recv, b_send, b_recv,
-           g1_send, g1_recv, g2_send, g2_recv, g3_send, g3_recv, k_send, k_recv):
+def sq_block(blk):
+    out = jnp.zeros((8, 128), F32)
+    sq = (blk * blk).reshape(16, 8, 512).sum(axis=0)
+    for i in range(4):
+        out = out + sq[:, i * 128:(i + 1) * 128]
+    return out
+
+
+def kernel(elem_count, wave_ref, left_ref, right_ref, two_ref, kr_ref, ab_ref,
+           slab, nslab, tmp, ut, u_ref, rin, rb, lb, wt, y_ref, z_ref, acc_o, acc_m, recv_s, recv_x, vecs, kbuf,
+           red_n, red_a, red_b,
+           ld_sem, sl_sem, r_send, r_recv, n_send, n_recv, s_send, s_recv, x_send, x_recv, a_send, a_recv,
+           b_send, b_recv, g1_send, g1_recv, g2_send, g2_recv, g3_send, g3_recv, k_send, k_recv):
     r = lax.axis_index('rows')
     c = lax.axis_index('terms')
     x = lax.rem(r, 4)
     y = lax.rem(r // 4, 4)
     z = r // 16
+    g = r // 4
     row_base = r - x
 
     def rcopy(src, dst, ssem, rsem, row, core):
         return pltpu.make_async_remote_copy(src_ref=src, dst_ref=dst, send_sem=ssem, recv_sem=rsem,
                                             device_id=(row, core), device_id_type=MESH)
 
-    cp_l = pltpu.make_async_copy(left_ref.at[:, pl.ds(pl.multiple_of(x * 128, 128), 128), :], lb, ld_sem.at[0])
-    cp_u = pltpu.make_async_copy(u0_ref, u_ref, ld_sem.at[1])
-    cp_r = pltpu.make_async_copy(right_ref, rin.at[x], ld_sem.at[2])
+    cp_r = pltpu.make_async_copy(right_ref, rin.at[x], ld_sem.at[0])
     cp_r.start()
-    cp_u.start()
+    n_loads, s_loads = [], []
+    for p in range(16):
+        rows_n = pl.ds(pl.multiple_of(z * 128, 128), 128)
+        n_loads.append(pltpu.make_async_copy(wave_ref.at[rows_n, p // 4, p % 4, :], nslab.at[p], sl_sem.at[0, p]))
+    for p in range(16):
+        rows_s = pl.ds(pl.multiple_of(x * 128, 128), 128)
+        s_loads.append(pltpu.make_async_copy(wave_ref.at[rows_s, p // 4, p % 4, :], slab.at[p], sl_sem.at[1, p]))
+    cp_l = pltpu.make_async_copy(left_ref.at[:, pl.ds(pl.multiple_of(x * 128, 128), 128), :], lb, ld_sem.at[1])
+    for cp in n_loads + s_loads:
+        cp.start()
     cp_l.start()
     cp_r.wait()
-    r_copies = []
+
+    right = row_base + lax.rem(x + 1, 4)
+    left = row_base + lax.rem(x + 3, 4)
+    xl = lax.rem(x + 3, 4)
+    xr = lax.rem(x + 1, 4)
+    halves = [pl.ds(0, 256), pl.ds(256, 256)]
+
+    def r_move(i, block, half, row):
+        ref = rin.at[block, halves[half], :]
+        return rcopy(ref, ref, r_send.at[i], r_recv.at[i], row, c)
+
+    r0 = r_move(0, x, 0, right)
+    r1 = r_move(1, x, 1, left)
+    r2 = r_move(2, x, 1, right)
+    r3 = r_move(3, x, 0, left)
+    r4 = r_move(4, xl, 0, right)
+    r5 = r_move(5, xr, 1, left)
+    for cp in (r0, r1, r2, r3):
+        cp.start()
+
+    for cp in n_loads:
+        cp.wait()
+
+    ssq = jnp.zeros((8, 128), F32)
+    ssq = lax.fori_loop(0, 16, lambda p, acc: acc + sq_block(nslab[p]), ssq)
+    red_n[0] = jnp.zeros((8, 128), F32) + total(ssq)
+    n_copies = []
     for d in range(1, 4):
-        px = lax.rem(x + d, 4)
-        cp = rcopy(rin.at[x], rin.at[x], r_send.at[d - 1], r_recv.at[d - 1], row_base + px, c)
+        row = lax.rem(z + d, 4) * 16 + y * 4 + x
+        cp = rcopy(red_n.at[0], red_n.at[d], n_send.at[d - 1], n_recv.at[d - 1], row, c)
         cp.start()
-        r_copies.append(cp)
+        n_copies.append(cp)
 
     lane16 = lax.broadcasted_iota(jnp.int32, (16, 256), 1)
     row16 = lax.broadcasted_iota(jnp.int32, (16, 256), 0)
@@ -67,11 +110,51 @@
         return carry
 
     lax.fori_loop(0, NT, build_w, 0)
-
-    vecs[0] = v0_ref[...]
-    kbuf[0] = kr0_ref[...]
-    for cp in r_copies:
+    r0.wait_recv()
+    r4.start()
+    r1.wait_recv()
+    r5.start()
+
+    for cp in n_copies:
         cp.wait()
+    norm = [red_n[lax.rem(z - s + 4, 4)] for s in range(4)]
+    scale = jnp.sqrt(((norm[0] + norm[1]) + (norm[2] + norm[3]))[:1, :1] / elem_count)
+    for cp in s_loads:
+        cp.wait()
+    b_lanes = pl.ds(pl.multiple_of((g // 4) * 128, 128), 128)
+    b_rows = pl.ds(pl.multiple_of(lax.rem(g, 4) * 32 + c * 16, 16), 16)
+
+    def first(p, carry):
+        ut[p] = (slab[p] / scale).astype(BF16)
+        tmp[...] = jnp.transpose(slab[p, :, b_lanes])
+        vecs[0, pl.ds(pl.multiple_of(p * 16, 16), 16), :] = tmp[b_rows, :] / scale
+        return carry
+
+    lax.fori_loop(0, 16, first, 0)
+
+    out_lanes = pl.ds(pl.multiple_of(lax.rem(x, 2) * 128, 128), 128)
+
+    def piece(jv, h):
+        return vecs.at[jv].reshape(16, 16, 128).at[:, h * 8:(h + 1) * 8, :]
+
+    def emit(jv):
+        for h in range(2):
+            dst_x = 2 * c + h
+            dst_c = x // 2
+            is_me = jnp.logical_and(dst_x == x, dst_c == c)
+
+            @pl.when(jnp.logical_not(is_me))
+            def _():
+                rcopy(piece(jv, h), kbuf.at[jv, :, :, out_lanes], k_send.at[jv, h], k_recv.at[jv, lax.rem(x, 2)],
+                      row_base + dst_x, dst_c).start()
+
+            @pl.when(is_me)
+            def _():
+                kbuf[jv, :, :, out_lanes] = vecs[jv].reshape(16, 16, 128)[:, h * 8:(h + 1) * 8, :]
+
+    for cp in (r2, r3, r4, r5):
+        cp.wait_recv()
+    emit(0)
 
     def build_r(i, carry):
         rows = pl.ds(pl.multiple_of(i * 64, 64), 64)
@@ -83,7 +166,32 @@
         return carry
 
     lax.fori_loop(0, 8, build_r, 0)
-    cp_u.wait()
+    for cp in (r0, r1, r2, r3, r4, r5):
+        cp.wait_send()
+
+    def put_y(o, bhi, mc, pp):
+        o = o.astype(BF16).reshape(32, 16, 256)
+        y_ref[mc * 32:(mc + 1) * 32, bhi, 2 * pp] = o[:, :, :128]
+        y_ref[mc * 32:(mc + 1) * 32, bhi, 2 * pp + 1] = o[:, :, 128:]
+
+    def s1_first(pp, carry):
+        w = ut[pl.ds(2 * pp, 2)].reshape(256, 512)
+        for bhi in range(2):
+            for mc in range(2):
+                o = lax.dot_general(rb[bhi, mc * 512:(mc + 1) * 512, :], w, (((1,), (1,)), ((), ())),
+                                    preferred_element_type=F32)
+                put_y(o, bhi, mc, pp)
+        return carry
+
+    def s1(pp, carry):
+        w = jnp.concatenate([u_ref[2 * pp].reshape(512, 128), u_ref[2 * pp + 1].reshape(512, 128)], axis=1)
+        for bhi in range(2):
+            for mc in range(2):
+                o = jnp.dot(rb[bhi, mc * 512:(mc + 1) * 512, :], w, preferred_element_type=F32)
+                put_y(o, bhi, mc, pp)
+        return carry
+
+    lax.fori_loop(0, 8, s1_first, 0)
     cp_l.wait()
 
     row_id = lax.broadcasted_iota(jnp.int32, (8, 128), 0)
@@ -108,18 +216,6 @@
         return col_sum(p), n_all, mean, r_all, col_sum(ss)
 
     def step(j, prev_beta):
-        def s1(pp, carry):
-            w = jnp.concatenate([u_ref[2 * pp].reshape(512, 128), u_ref[2 * pp + 1].reshape(512, 128)], axis=1)
-            for bhi in range(2):
-                for mc in range(2):
-                    o = jnp.dot(rb[bhi, mc * 512:(mc + 1) * 512, :], w, preferred_element_type=F32)
-                    o = o.astype(BF16).reshape(32, 16, 256)
-                    y_ref[mc * 32:(mc + 1) * 32, bhi, 2 * pp] = o[:, :, :128]
-                    y_ref[mc * 32:(mc + 1) * 32, bhi, 2 * pp + 1] = o[:, :, 128:]
-            return carry
-
-        lax.fori_loop(0, 8, s1, 0)
-
         def s2(kk, carry):
             for i in range(4):
                 k = kk * 4 + i
@@ -190,7 +286,6 @@
 
         red_b[0] = pack(*merge(*[gather_rows(blocks, i) for i in range(5)]))
         b_copies = []
-        g = z * 4 + y
         for d in range(1, 16):
             pg = lax.rem(g + d, 16)
             cp = rcopy(red_b.at[0], red_b.at[d], b_send.at[d - 1], b_recv.at[d - 1], pg * 4 + x, c)
@@ -211,21 +306,7 @@
         ab_ref[pl.ds(j, 1), :] = alpha
         ab_ref[pl.ds(8 + j, 1), :] = beta
 
-        for h in range(2):
-            dst_x = 2 * c + h
-            dst_c = x // 2
-            is_me = jnp.logical_and(dst_x == x, dst_c == c)
-            lanes = pl.ds(pl.multiple_of(lax.rem(x, 2) * 128, 128), 128)
-            src = vecs.at[j + 1].reshape(16, 16, 128).at[:, h * 8:(h + 1) * 8, :]
-
-            @pl.when(jnp.logical_not(is_me))
-            def _():
-                rcopy(src, kbuf.at[j + 1, :, :, lanes], k_send.at[j, h], k_recv.at[j, lax.rem(x, 2)],
-                      row_base + dst_x, dst_c).start()
-
-            @pl.when(is_me)
-            def _():
-                kbuf[j + 1, :, :, lanes] = v_new.reshape(16, 16, 128)[:, h * 8:(h + 1) * 8, :]
+        emit(j + 1)
 
         @pl.when(j < STEPS - 1)
         def _():
@@ -259,20 +340,20 @@
             cp3 = rcopy(s3_, s3_, g3_send.at[0], g3_recv.at[0], r, 1 - c)
             cp3.start()
             cp3.wait()
+            lax.fori_loop(0, 8, s1, 0)
 
         return beta_s
 
     lax.fori_loop(0, STEPS, step, jnp.zeros((1, 1), F32))
 
-    def drain(j, carry):
+    def drain(jv, carry):
         for h in range(2):
             dst_x = 2 * c + h
             dst_c = x // 2
-            src = vecs.at[j + 1].reshape(16, 16, 128).at[:, h * 8:(h + 1) * 8, :]
 
             @pl.when(jnp.logical_not(jnp.logical_and(dst_x == x, dst_c == c)))
             def _():
-                rcopy(src, kbuf.at[j + 1, :, :, 0:128], k_send.at[j, h], k_recv.at[j, 0],
+                rcopy(piece(jv, h), kbuf.at[jv, :, :, 0:128], k_send.at[jv, h], k_recv.at[jv, 0],
                       row_base + dst_x, dst_c).wait_send()
 
         for m in range(2):
@@ -281,12 +362,12 @@
 
             @pl.when(jnp.logical_not(jnp.logical_and(src_x == x, src_c == c)))
             def _():
-                rcopy(vecs.at[j + 1].reshape(16, 16, 128).at[:, 0:8, :], kbuf.at[j + 1, :, :, m * 128:(m + 1) * 128],
-                      k_send.at[j, 0], k_recv.at[j, m], row_base + src_x, src_c).wait_recv()
-
-        return carry
-
-    lax.fori_loop(0, STEPS, drain, 0)
+                rcopy(piece(jv, 0), kbuf.at[jv, :, :, m * 128:(m + 1) * 128], k_send.at[jv, 0], k_recv.at[jv, m],
+                      row_base + src_x, src_c).wait_recv()
+
+        return carry
+
+    lax.fori_loop(0, STEPS + 1, drain, 0)
     cp_k = pltpu.make_async_copy(kbuf, kr_ref, ld_sem.at[0])
     cp_k.start()
     cp_k.wait()
@@ -297,27 +378,19 @@
 
     def body_fn(wavefunc, left_loc, two_loc, right_loc):
         elem_count = float(wavefunc.size)
-        row = lax.axis_index('rows')
-        core = lax.axis_index('terms')
-        xi = lax.rem(row, 4)
-        gi = row // 4
-        wave = wavefunc.reshape(512, 16, 512)
-        scale = jnp.sqrt(jnp.mean(wave * wave))
-        slab = lax.dynamic_slice(wave, (xi * 128, 0, 0), (128, 16, 512)) / scale
-        u0 = jnp.transpose(slab.astype(BF16), (1, 2, 0)).reshape(16, 4, 4, 2, 16, 128)
-        mine = lax.dynamic_slice(slab, (0, 0, gi * 32 + core * 16), (128, 16, 16))
-        v0 = jnp.transpose(mine, (1, 2, 0)).reshape(256, 128)
-        out0 = lax.dynamic_slice(wave, (core * 256, 0, row * 8), (256, 16, 8)) / scale
-        kr0 = jnp.transpose(out0, (1, 2, 0))
         vm = pl.BlockSpec(memory_space=pltpu.VMEM)
         hbm = pl.BlockSpec(memory_space=pl.ANY)
         dma = pltpu.SemaphoreType.DMA
         kr, ab = pl.pallas_call(
             lambda *refs: kernel(elem_count, *refs),
             out_shape=(jax.ShapeDtypeStruct((STEPS + 1, 16, 8, 256), F32), jax.ShapeDtypeStruct((16, 128), F32)),
-            in_specs=[hbm, vm, vm, hbm, hbm, vm],
+            in_specs=[hbm, hbm, hbm, vm],
             out_specs=(hbm, vm),
             scratch_shapes=[
+                pltpu.VMEM((16, 128, 512), F32),
+                pltpu.VMEM((16, 128, 512), F32),
+                pltpu.VMEM((128, 128), F32),
+                pltpu.VMEM((16, 128, 512), BF16),
                 pltpu.VMEM((16, 4, 4, 2, 16, 128), BF16),
                 pltpu.VMEM((4, 512, 512), BF16),
                 pltpu.VMEM((2, 1024, 512), BF16),
@@ -331,15 +404,16 @@
                 pltpu.VMEM((3, 256, 128), F32),
                 pltpu.VMEM((STEPS + 1, 256, 128), F32),
                 pltpu.VMEM((STEPS + 1, 16, 8, 256), F32),
+                pltpu.VMEM((4, 8, 128), F32),
                 pltpu.VMEM((8, 8, 128), F32),
                 pltpu.VMEM((16, 8, 128), F32),
-                dma((3,)), dma((3,)), dma((3,)), dma((1,)), dma((1,)), dma((3,)), dma((3,)),
+                dma((2,)), dma((2, 16)), dma((6,)), dma((6,)), dma((3,)), dma((3,)), dma((1,)), dma((1,)), dma((3,)), dma((3,)),
                 dma((7,)), dma((7,)), dma((15,)), dma((15,)),
                 dma((2, 3)), dma((2, 3)), dma((2, 3)), dma((2, 3)), dma((1,)), dma((1,)),
-                dma((STEPS, 2)), dma((STEPS, 2)),
+                dma((STEPS + 1, 2)), dma((STEPS + 1, 2)),
             ],
             compiler_params=pltpu.CompilerParams(has_side_effects=True, vmem_limit_bytes=60 * 1024 * 1024),
-        )(u0, v0, kr0, left_loc, right_loc.reshape(512, 512), two_loc.reshape(1024, 16))
+        )(wavefunc, left_loc, right_loc.reshape(512, 512), two_loc.reshape(1024, 16))
         krylov = jnp.transpose(kr.reshape(STEPS + 1, 4, 4, 8, 256), (0, 4, 1, 2, 3))
         return krylov, ab[:STEPS, 0], ab[8:8 + STEPS, 0]
 

time: 370 us -> 334 us (0.903)
  local copies, waits for them, and re-layouts: 25.3 us -> 5.31 us
  other arithmetic: 18.1 us -> 0 us
  Pallas kernels: 324 us -> 328 us
    unnamed x5 -> x2, local copies, waits for them, and re-layouts: 22.4 us -> 3.97 us
    reduce_sum x1 -> x0, other arithmetic: 10.9 us -> none  [body_fn(): scale = jnp.sqrt(jnp.mean(wave * wave))]
    convert_element_type x1 -> x0, other arithmetic: 5.63 us -> none  [body_fn(): slab.astype(BF16)]
    pallas_call x1, Pallas kernels: 324 us -> 328 us  [body_fn(): pl.pallas_call(lambda *refs: kernel(elem_count, *refs), out_shape=(jax.Sh...]
where the time goes in v2:
time: 334 us
  Pallas kernels  328 us (98%)
  local copies, waits for them, and re-layouts  5.31 us (2%)
    pallas_call x1, Pallas kernels, body_fn(): pl.pallas_call(lambda *refs: kernel(elem_count, *refs), out_shape=(jax.Sh...  328 us

profile of v2, /device:TPU:1, one launch (start us, length us, event | category | flops | bytes accessed | tf_op | source)
XLA Modules:
  0.0 334.1 jit_solution(17160912674783463303)
XLA Ops:
  0.6 1.8 copy.8
  2.4 328.2 %shard_map.67 = (f32[7,16,8,256]{3,2,1,0:T(8,128)}, f32[16,128]{1,0:T(8,128)}) custom-call(f32[512,4,4,512]{3,2,1,0:T(4,128)} %refs_0_.1, bf16[64,512,512]{2,1,0:T(8,128)(2,1)} %refs_1_.1, bf16[512,512]{1,0:T(8,128)(2,1)} %bitcast.7, bf16[1024,16]{1,0:T(8,128)(2,1)} %bitcast.5), custom_call_target="tpu_custom_call" | custom-call | tf_op jit(solution)/shard_map/pallas_call | solution.py:384
  330.6 1.3 slice_reduce_fusion
  331.9 2.2 copy.10

commit v3 on v2

--- a/solution.py
+++ b/solution.py
@@ -40,6 +40,12 @@
     z = r // 16
     g = r // 4
     row_base = r - x
+    z_peers = [lax.rem(z + d, 4) * 16 + y * 4 + x for d in (1, 2, 3)]
+    y_peers = [z * 16 + lax.rem(y + d, 4) * 4 + x for d in (1, 2, 3)]
+    x_peers = [row_base + lax.rem(x + d, 4) for d in (1, 2, 3)]
+
+    def pair(i, h):
+        return pl.ds(8 * h + 2 * i, 2)
 
     def rcopy(src, dst, ssem, rsem, row, core):
         return pltpu.make_async_remote_copy(src_ref=src, dst_ref=dst, send_sem=ssem, recv_sem=rsem,
@@ -86,9 +92,8 @@
     ssq = lax.fori_loop(0, 16, lambda p, acc: acc + sq_block(nslab[p]), ssq)
     red_n[0] = jnp.zeros((8, 128), F32) + total(ssq)
     n_copies = []
-    for d in range(1, 4):
-        row = lax.rem(z + d, 4) * 16 + y * 4 + x
-        cp = rcopy(red_n.at[0], red_n.at[d], n_send.at[d - 1], n_recv.at[d - 1], row, c)
+    for d, row in enumerate(z_peers):
+        cp = rcopy(red_n.at[0], red_n.at[d + 1], n_send.at[d], n_recv.at[d], row, c)
         cp.start()
         n_copies.append(cp)
 
@@ -253,9 +258,8 @@
         for i in range(4):
             acc_m[i] += recv_s[i]
         x_copies = []
-        for d in range(1, 4):
-            px = lax.rem(x + d, 4)
-            cp = rcopy(acc_m.at[px], recv_x.at[d - 1], x_send.at[d - 1], x_recv.at[d - 1], row_base + px, c)
+        for d, row in enumerate(x_peers):
+            cp = rcopy(acc_m.at[row - row_base], recv_x.at[d], x_send.at[d], x_recv.at[d], row, c)
             cp.start()
             x_copies.append(cp)
         for cp in x_copies:
@@ -311,36 +315,52 @@
         @pl.when(j < STEPS - 1)
         def _():
             u_ref[:, z, y, c] = v_new.astype(BF16).reshape(16, 16, 128)
-            lo, hi = pl.ds(0, 8), pl.ds(8, 8)
-            cps = []
-            for d in range(1, 4):
-                zrow = lax.rem(z + d, 4) * 16 + y * 4 + x
-                yrow = z * 16 + lax.rem(y + d, 4) * 4 + x
-                s1_ = u_ref.at[lo, z, y, c]
-                s2_ = u_ref.at[hi, z, y, c]
-                cps.append(rcopy(s1_, s1_, g1_send.at[0, d - 1], g1_recv.at[0, d - 1], zrow, c))
-                cps.append(rcopy(s2_, s2_, g1_send.at[1, d - 1], g1_recv.at[1, d - 1], yrow, c))
-            for cp in cps:
-                cp.start()
-            for cp in cps:
-                cp.wait()
-            cps = []
-            for d in range(1, 4):
-                zrow = lax.rem(z + d, 4) * 16 + y * 4 + x
-                yrow = z * 16 + lax.rem(y + d, 4) * 4 + x
-                s1_ = u_ref.at[lo, :, y, c]
-                s2_ = u_ref.at[hi, z, :, c]
-                cps.append(rcopy(s1_, s1_, g2_send.at[0, d - 1], g2_recv.at[0, d - 1], yrow, c))
-                cps.append(rcopy(s2_, s2_, g2_send.at[1, d - 1], g2_recv.at[1, d - 1], zrow, c))
-            for cp in cps:
-                cp.start()
-            for cp in cps:
-                cp.wait()
-            s3_ = u_ref.at[:, :, :, c]
-            cp3 = rcopy(s3_, s3_, g3_send.at[0], g3_recv.at[0], r, 1 - c)
-            cp3.start()
-            cp3.wait()
-            lax.fori_loop(0, 8, s1, 0)
+            moves = [(h, d) for h in range(2) for d in range(3)]
+            cuts = range(4)
+
+            def move(sems, h, i, d, ref, across):
+                row = z_peers[d] if across else y_peers[d]
+                return rcopy(ref, ref, sems[0].at[h, i, d], sems[1].at[h, i, d], row, c)
+
+            def p1(i, h, d):
+                ref = u_ref.at[pair(i, h), z, y, c]
+                return move((g1_send, g1_recv), h, i, d, ref, h == 0)
+
+            def p2(i, h, d):
+                ref = u_ref.at[pair(i, h), z, :, c] if h else u_ref.at[pair(i, h), :, y, c]
+                return move((g2_send, g2_recv), h, i, d, ref, h == 1)
+
+            def p3(i, h):
+                ref = u_ref.at[pair(i, h), :, :, c]
+                return rcopy(ref, ref, g3_send.at[h, i], g3_recv.at[h, i], r, 1 - c)
+
+            def product(i):
+                for h in range(2):
+                    p3(i, h).wait_recv()
+                lax.fori_loop(0, 2, lambda h, carry: s1(4 * h + i, carry), 0)
+
+            for i in cuts:
+                for h, d in moves:
+                    p1(i, h, d).start()
+            for i in cuts:
+                for h, d in moves:
+                    p1(i, h, d).wait_recv()
+                for h, d in moves:
+                    p2(i, h, d).start()
+            for i in cuts:
+                for h, d in moves:
+                    p2(i, h, d).wait_recv()
+                for h in range(2):
+                    p3(i, h).start()
+                if i:
+                    product(i - 1)
+            product(cuts[-1])
+            for i in cuts:
+                for h, d in moves:
+                    p1(i, h, d).wait_send()
+                    p2(i, h, d).wait_send()
+                for h in range(2):
+                    p3(i, h).wait_send()
 
         return beta_s
 
@@ -409,7 +429,7 @@
                 pltpu.VMEM((16, 8, 128), F32),
                 dma((2,)), dma((2, 16)), dma((6,)), dma((6,)), dma((3,)), dma((3,)), dma((1,)), dma((1,)), dma((3,)), dma((3,)),
                 dma((7,)), dma((7,)), dma((15,)), dma((15,)),
-                dma((2, 3)), dma((2, 3)), dma((2, 3)), dma((2, 3)), dma((1,)), dma((1,)),
+                dma((2, 4, 3)), dma((2, 4, 3)), dma((2, 4, 3)), dma((2, 4, 3)), dma((2, 4)), dma((2, 4)),
                 dma((STEPS + 1, 2)), dma((STEPS + 1, 2)),
             ],
             compiler_params=pltpu.CompilerParams(has_side_effects=True, vmem_limit_bytes=60 * 1024 * 1024),

time: 334 us -> 317 us (0.949)
  Pallas kernels: 328 us -> 311 us
    pallas_call x1, Pallas kernels: 328 us -> 311 us  [body_fn(): pl.pallas_call(lambda *refs: kernel(elem_count, *refs), out_shape=(jax.Sh...]
where the time goes in v3:
time: 317 us
  Pallas kernels  311 us (98%)
  local copies, waits for them, and re-layouts  5.31 us (2%)
    pallas_call x1, Pallas kernels, body_fn(): pl.pallas_call(lambda *refs: kernel(elem_count, *refs), out_shape=(jax.Sh...  311 us

profile of v3, /device:TPU:1, one launch (start us, length us, event | category | flops | bytes accessed | tf_op | source)
XLA Modules:
  0.0 316.7 jit_solution(9090884058822748256)
XLA Ops:
  0.6 1.8 copy.8
  2.4 310.8 %shard_map.67 = (f32[7,16,8,256]{3,2,1,0:T(8,128)}, f32[16,128]{1,0:T(8,128)}) custom-call(f32[512,4,4,512]{3,2,1,0:T(4,128)} %refs_0_.1, bf16[64,512,512]{2,1,0:T(8,128)(2,1)} %refs_1_.1, bf16[512,512]{1,0:T(8,128)(2,1)} %bitcast.7, bf16[1024,16]{1,0:T(8,128)(2,1)} %bitcast.5), custom_call_target="tpu_custom_call" | custom-call | tf_op jit(solution)/shard_map/pallas_call | solution.py:404
  313.2 1.3 slice_reduce_fusion
  314.5 2.2 copy.10

commit v4 on v3

--- a/solution.py
+++ b/solution.py
@@ -16,6 +16,10 @@
     return jnp.sum(jnp.sum(x, axis=1, keepdims=True), axis=0, keepdims=True)
 
 
+def blk(i, size):
+    return pl.ds(pl.multiple_of(i * size, size), size)
+
+
 def col_sum(x):
     return jnp.sum(x, axis=0, keepdims=True)
 
@@ -29,7 +33,7 @@
 
 
 def kernel(elem_count, wave_ref, left_ref, right_ref, two_ref, kr_ref, ab_ref,
-           slab, nslab, tmp, ut, u_ref, rin, rb, lb, wt, y_ref, z_ref, acc_o, acc_m, recv_s, recv_x, vecs, kbuf,
+           slab, nslab, tmp, wide, ut, u_ref, rin, rb, lb, wt, y_ref, z_ref, acc, recv_s, recv_x, vecs, kbuf,
            red_n, red_a, red_b,
            ld_sem, sl_sem, r_send, r_recv, n_send, n_recv, s_send, s_recv, x_send, x_recv, a_send, a_recv,
            b_send, b_recv, g1_send, g1_recv, g2_send, g2_recv, g3_send, g3_recv, k_send, k_recv):
@@ -51,20 +55,28 @@
         return pltpu.make_async_remote_copy(src_ref=src, dst_ref=dst, send_sem=ssem, recv_sem=rsem,
                                             device_id=(row, core), device_id_type=MESH)
 
+    me = x * 2 + c
+    group = [(row_base + lax.rem(me + d, 8) // 2, lax.rem(me + d, 2)) for d in range(1, 8)]
+    plane = [(lax.rem(g + d, 16) * 4 + x, c) for d in range(1, 16)]
+    barrier = pltpu.get_barrier_semaphore()
+    for peer in group + plane:
+        pl.semaphore_signal(barrier, inc=1, device_id=peer, device_id_type=MESH)
+
     cp_r = pltpu.make_async_copy(right_ref, rin.at[x], ld_sem.at[0])
     cp_r.start()
     n_loads, s_loads = [], []
     for p in range(16):
-        rows_n = pl.ds(pl.multiple_of(z * 128, 128), 128)
+        rows_n = blk(z, 128)
         n_loads.append(pltpu.make_async_copy(wave_ref.at[rows_n, p // 4, p % 4, :], nslab.at[p], sl_sem.at[0, p]))
     for p in range(16):
-        rows_s = pl.ds(pl.multiple_of(x * 128, 128), 128)
+        rows_s = blk(x, 128)
         s_loads.append(pltpu.make_async_copy(wave_ref.at[rows_s, p // 4, p % 4, :], slab.at[p], sl_sem.at[1, p]))
-    cp_l = pltpu.make_async_copy(left_ref.at[:, pl.ds(pl.multiple_of(x * 128, 128), 128), :], lb, ld_sem.at[1])
+    cp_l = pltpu.make_async_copy(left_ref.at[:, blk(x, 128), :], lb, ld_sem.at[1])
     for cp in n_loads + s_loads:
         cp.start()
     cp_l.start()
     cp_r.wait()
+    pl.semaphore_wait(barrier, len(group) + len(plane))
 
     right = row_base + lax.rem(x + 1, 4)
     left = row_base + lax.rem(x + 3, 4)
@@ -107,14 +119,17 @@
     lane_m = lax.broadcasted_iota(jnp.int32, (256, 256), 1)
     diag = lax.rem(row_m, 16) == lax.rem(lane_m, 16)
 
-    def build_w(k, carry):
-        wk = two_ref[pl.ds(pl.multiple_of(k * 16, 16), 16), :]
-        wide = jnp.dot(wk, e_col, preferred_element_type=F32).astype(BF16)
-        full = jnp.dot(e_row, wide, preferred_element_type=F32)
-        wt[k] = jnp.where(diag, full, 0.0).astype(BF16)
+    wide[...] = jnp.dot(two_ref[...], e_col, preferred_element_type=F32).astype(BF16)
+
+    def build_w(kk, carry):
+        for i in range(8):
+            k = kk * 8 + i
+            rows = wide[blk(k, 16), :]
+            full = jnp.dot(e_row, rows, preferred_element_type=F32)
+            wt[k] = jnp.where(diag, full, 0.0).astype(BF16)
         return carry
 
-    lax.fori_loop(0, NT, build_w, 0)
+    lax.fori_loop(0, NT // 8, build_w, 0)
     r0.wait_recv()
     r4.start()
     r1.wait_recv()
@@ -126,18 +141,18 @@
     scale = jnp.sqrt(((norm[0] + norm[1]) + (norm[2] + norm[3]))[:1, :1] / elem_count)
     for cp in s_loads:
         cp.wait()
-    b_lanes = pl.ds(pl.multiple_of((g // 4) * 128, 128), 128)
-    b_rows = pl.ds(pl.multiple_of(lax.rem(g, 4) * 32 + c * 16, 16), 16)
+    b_lanes = blk(g // 4, 128)
+    b_rows = blk(lax.rem(g, 4) * 2 + c, 16)
 
     def first(p, carry):
         ut[p] = (slab[p] / scale).astype(BF16)
         tmp[...] = jnp.transpose(slab[p, :, b_lanes])
-        vecs[0, pl.ds(pl.multiple_of(p * 16, 16), 16), :] = tmp[b_rows, :] / scale
+        vecs[0, blk(p, 16), :] = tmp[b_rows, :] / scale
         return carry
 
     lax.fori_loop(0, 16, first, 0)
 
-    out_lanes = pl.ds(pl.multiple_of(lax.rem(x, 2) * 128, 128), 128)
+    out_lanes = blk(lax.rem(x, 2), 128)
 
     def piece(jv, h):
         return vecs.at[jv].reshape(16, 16, 128).at[:, h * 8:(h + 1) * 8, :]
@@ -157,46 +172,53 @@
             def _():
                 kbuf[jv, :, :, out_lanes] = vecs[jv].reshape(16, 16, 128)[:, h * 8:(h + 1) * 8, :]
 
-    for cp in (r2, r3, r4, r5):
-        cp.wait_recv()
-    emit(0)
-
-    def build_r(i, carry):
-        rows = pl.ds(pl.multiple_of(i * 64, 64), 64)
-        for bhi in range(2):
+    def build_r(bhi):
+        def body(i, carry):
+            rows = blk(i, 64)
             lo = rin[2 * bhi, rows, :].astype(F32).reshape(8, 8, 512)
             hi = rin[2 * bhi + 1, rows, :].astype(F32).reshape(8, 8, 512)
             both = jnp.concatenate([lo, hi], axis=1).reshape(128, 512)
-            rb[bhi, pl.ds(pl.multiple_of(i * 128, 128), 128), :] = both.astype(BF16)
-        return carry
-
-    lax.fori_loop(0, 8, build_r, 0)
+            rb[bhi, blk(i, 128), :] = both.astype(BF16)
+            return carry
+
+        lax.fori_loop(0, 8, body, 0)
+
+    def put_y(o, bhi, mc, pp):
+        o = o.astype(BF16).reshape(32, 16, 256)
+        rows = pl.ds(mc * 32, 32)
+        y_ref[rows, bhi, 2 * pp] = o[:, :, :128]
+        y_ref[rows, bhi, 2 * pp + 1] = o[:, :, 128:]
+
+    def s1_first(bhi):
+        def body(i, carry):
+            for pp in (i, i + 4):
+                w = ut[pl.ds(2 * pp, 2)].reshape(256, 512)
+                for mc in range(2):
+                    rows = rb[bhi, pl.ds(mc * 512, 512), :]
+                    o = lax.dot_general(rows, w, (((1,), (1,)), ((), ())), preferred_element_type=F32)
+                    put_y(o, bhi, mc, pp)
+            return carry
+
+        lax.fori_loop(0, 4, body, 0)
+
+    def s1(pp):
+        w = jnp.concatenate([u_ref[2 * pp + i].reshape(512, 128) for i in range(2)], axis=1)
+        for bhi in range(2):
+            for mc in range(2):
+                put_y(jnp.dot(rb[bhi, pl.ds(mc * 512, 512), :], w, preferred_element_type=F32), bhi, mc, pp)
+
+    for cp in (r2, r3):
+        cp.wait_recv()
+    emit(0)
+    own = x // 2
+    build_r(own)
+    s1_first(own)
+    for cp in (r4, r5):
+        cp.wait_recv()
+    build_r(1 - own)
+    s1_first(1 - own)
     for cp in (r0, r1, r2, r3, r4, r5):
         cp.wait_send()
-
-    def put_y(o, bhi, mc, pp):
-        o = o.astype(BF16).reshape(32, 16, 256)
-        y_ref[mc * 32:(mc + 1) * 32, bhi, 2 * pp] = o[:, :, :128]
-        y_ref[mc * 32:(mc + 1) * 32, bhi, 2 * pp + 1] = o[:, :, 128:]
-
-    def s1_first(pp, carry):
-        w = ut[pl.ds(2 * pp, 2)].reshape(256, 512)
-        for bhi in range(2):
-            for mc in range(2):
-                o = lax.dot_general(rb[bhi, mc * 512:(mc + 1) * 512, :], w, (((1,), (1,)), ((), ())),
-                                    preferred_element_type=F32)
-                put_y(o, bhi, mc, pp)
-        return carry
-
-    def s1(pp, carry):
-        w = jnp.concatenate([u_ref[2 * pp].reshape(512, 128), u_ref[2 * pp + 1].reshape(512, 128)], axis=1)
-        for bhi in range(2):
-            for mc in range(2):
-                o = jnp.dot(rb[bhi, mc * 512:(mc + 1) * 512, :], w, preferred_element_type=F32)
-                put_y(o, bhi, mc, pp)
-        return carry
-
-    lax.fori_loop(0, 8, s1_first, 0)
     cp_l.wait()
 
     row_id = lax.broadcasted_iota(jnp.int32, (8, 128), 0)
@@ -222,49 +244,60 @@
 
     def step(j, prev_beta):
         def s2(kk, carry):
-            for i in range(4):
-                k = kk * 4 + i
+            for i in range(16):
+                k = kk * 16 + i
                 rhs = jnp.concatenate([y_ref[k, 0].reshape(256, 128), y_ref[k, 1].reshape(256, 128)], axis=1)
                 o = jnp.dot(wt[k], rhs, preferred_element_type=F32).astype(BF16)
                 z_ref[0, k] = o[:, :128]
                 z_ref[1, k] = o[:, 128:]
             return carry
 
-        lax.fori_loop(0, NT // 4, s2, 0)
-
-        def s3(bhi, acc):
-            def part(kc):
-                lhs = jnp.concatenate([z_ref[bhi, kc * 8 + i] for i in range(8)], axis=1)
-                rhs = lb[pl.ds(kc * 8, 8)].reshape(1024, 512)
-                return jnp.dot(lhs, rhs, preferred_element_type=F32)
-
-            o = part(0)
-            for i in range(4):
-                acc[i] = o[:, i * 128:(i + 1) * 128]
-
-            def more(kc, carry):
-                o = part(kc)
-                for i in range(4):
-                    acc[i] += o[:, i * 128:(i + 1) * 128]
-                return carry
-
-            lax.fori_loop(1, 8, more, 0)
-
-        s3(1 - c, acc_o)
-        cp_s = rcopy(acc_o, recv_s, s_send.at[0], s_recv.at[0], r, 1 - c)
-        cp_s.start()
-        s3(c, acc_m)
-        cp_s.wait()
-        for i in range(4):
-            acc_m[i] += recv_s[i]
+        lax.fori_loop(0, NT // 16, s2, 0)
+
+
+        order = [lax.rem(x + d, 4) for d in (2, 1, 3, 0)]
+
+        def s3(lo, first_k, count):
+            slices = [blk(pos, 128) for pos in order[lo:lo + 2]]
+            outs = [None, None]
+            for k0 in range(first_k, first_k + count, 8):
+                rhs = jnp.concatenate([lb[pl.ds(k0, 8), :, sl].reshape(1024, 128) for sl in slices], axis=1)
+                for bhi in range(2):
+                    lhs = jnp.concatenate([z_ref[bhi, k0 + k] for k in range(8)], axis=1)
+                    o = jnp.dot(lhs, rhs, preferred_element_type=F32)
+                    outs[bhi] = o if outs[bhi] is None else outs[bhi] + o
+            for n in range(2):
+                for bhi in range(2):
+                    part = outs[bhi][:, n * 128:(n + 1) * 128]
+                    acc[bhi, lo + n] = acc[bhi, lo + n] + part if first_k else part
+
+        acc_o = acc.at[1 - c]
+        acc_m = acc.at[c]
+        s_copies = []
+        for n in range(2):
+            two = pl.ds(2 * n, 2)
+            s_copies.append(rcopy(acc_o.at[two], recv_s.at[two], s_send.at[n], s_recv.at[n], r, 1 - c))
         x_copies = []
-        for d, row in enumerate(x_peers):
-            cp = rcopy(acc_m.at[row - row_base], recv_x.at[d], x_send.at[d], x_recv.at[d], row, c)
-            cp.start()
-            x_copies.append(cp)
+        for n in range(3):
+            x_copies.append(rcopy(acc_m.at[n], recv_x.at[n], x_send.at[n], x_recv.at[n], row_base + order[n], c))
+        s3(0, 0, NT)
+        s_copies[0].start()
+        s3(2, 0, NT // 2)
+        s_copies[0].wait_recv()
+        for n in range(2):
+            acc_m[n] += recv_s[n]
+            x_copies[n].start()
+        s3(2, NT // 2, NT // 2)
+        s_copies[1].start()
+        s_copies[1].wait_recv()
+        acc_m[2] += recv_s[2]
+        x_copies[2].start()
+        w_own = acc_m[3] + recv_s[3]
+        for cp in s_copies:
+            cp.wait_send()
         for cp in x_copies:
             cp.wait()
-        w_vec = (acc_m[x] + recv_x[0]) + (recv_x[1] + recv_x[2])
+        w_vec = (w_own + recv_x[0]) + (recv_x[1] + recv_x[2])
         v_cur = vecs[j]
         v_old = vecs[lax.max(j - 1, 0)]
 
@@ -274,27 +307,20 @@
         e_loc = w_res - a_loc * v_cur
         red_a[0] = pack(total(w_vec * v_cur), n_loc, a_loc, total(e_loc * e_loc), total(e_loc * v_cur))
 
-        a_copies = []
-        for d in range(1, 8):
-            slot = lax.rem(x * 2 + c + d, 8)
-            cp = rcopy(red_a.at[0], red_a.at[d], a_send.at[d - 1], a_recv.at[d - 1], row_base + slot // 2, lax.rem(slot, 2))
+        a_copies = [rcopy(red_a.at[0], red_a.at[d + 1], a_send.at[d], a_recv.at[d], *peer) for d, peer in enumerate(group)]
+        for cp in a_copies:
             cp.start()
-            a_copies.append(cp)
         for cp in a_copies:
             cp.wait()
-        me = x * 2 + c
         blocks = [red_a[lax.rem(me - s + 8, 8)] for s in range(8)]
 
         def gather_rows(blks, i):
             return jnp.concatenate([bk[i:i + 1, :] for bk in blks], axis=0)
 
         red_b[0] = pack(*merge(*[gather_rows(blocks, i) for i in range(5)]))
-        b_copies = []
-        for d in range(1, 16):
-            pg = lax.rem(g + d, 16)
-            cp = rcopy(red_b.at[0], red_b.at[d], b_send.at[d - 1], b_recv.at[d - 1], pg * 4 + x, c)
+        b_copies = [rcopy(red_b.at[0], red_b.at[d + 1], b_send.at[d], b_recv.at[d], *peer) for d, peer in enumerate(plane)]
+        for cp in b_copies:
             cp.start()
-            b_copies.append(cp)
         for cp in b_copies:
             cp.wait()
         blocks = [red_b[lax.rem(g - s + 16, 16)] for s in range(16)]
@@ -337,7 +363,8 @@
             def product(i):
                 for h in range(2):
                     p3(i, h).wait_recv()
-                lax.fori_loop(0, 2, lambda h, carry: s1(4 * h + i, carry), 0)
+                s1(i)
+                s1(4 + i)
 
             for i in cuts:
                 for h, d in moves:
@@ -410,6 +437,7 @@
                 pltpu.VMEM((16, 128, 512), F32),
                 pltpu.VMEM((16, 128, 512), F32),
                 pltpu.VMEM((128, 128), F32),
+                pltpu.VMEM((1024, 256), BF16),
                 pltpu.VMEM((16, 128, 512), BF16),
                 pltpu.VMEM((16, 4, 4, 2, 16, 128), BF16),
                 pltpu.VMEM((4, 512, 512), BF16),
@@ -418,8 +446,7 @@
                 pltpu.VMEM((NT, 256, 256), BF16),
                 pltpu.VMEM((NT, 2, 16, 16, 128), BF16),
                 pltpu.VMEM((2, NT, 256, 128), BF16),
-                pltpu.VMEM((4, 256, 128), F32),
-                pltpu.VMEM((4, 256, 128), F32),
+                pltpu.VMEM((2, 4, 256, 128), F32),
                 pltpu.VMEM((4, 256, 128), F32),
                 pltpu.VMEM((3, 256, 128), F32),
                 pltpu.VMEM((STEPS + 1, 256, 128), F32),
@@ -427,12 +454,12 @@
                 pltpu.VMEM((4, 8, 128), F32),
                 pltpu.VMEM((8, 8, 128), F32),
                 pltpu.VMEM((16, 8, 128), F32),
-                dma((2,)), dma((2, 16)), dma((6,)), dma((6,)), dma((3,)), dma((3,)), dma((1,)), dma((1,)), dma((3,)), dma((3,)),
+                dma((2,)), dma((2, 16)), dma((6,)), dma((6,)), dma((3,)), dma((3,)), dma((2,)), dma((2,)), dma((3,)), dma((3,)),
                 dma((7,)), dma((7,)), dma((15,)), dma((15,)),
                 dma((2, 4, 3)), dma((2, 4, 3)), dma((2, 4, 3)), dma((2, 4, 3)), dma((2, 4)), dma((2, 4)),
                 dma((STEPS + 1, 2)), dma((STEPS + 1, 2)),
             ],
-            compiler_params=pltpu.CompilerParams(has_side_effects=True, vmem_limit_bytes=60 * 1024 * 1024),
+            compiler_params=pltpu.CompilerParams(has_side_effects=True, collective_id=0, vmem_limit_bytes=60 * 1024 * 1024),
         )(wavefunc, left_loc, right_loc.reshape(512, 512), two_loc.reshape(1024, 16))
         krylov = jnp.transpose(kr.reshape(STEPS + 1, 4, 4, 8, 256), (0, 4, 1, 2, 3))
         return krylov, ab[:STEPS, 0], ab[8:8 + STEPS, 0]

time: 317 us -> 262 us (0.83)
  Pallas kernels: 311 us -> 256 us
    pallas_call x1, Pallas kernels: 311 us -> 256 us  [body_fn(): pl.pallas_call(lambda *refs: kernel(elem_count, *refs), out_shape=(jax.Sh...]
where the time goes in v4:
time: 262 us
  Pallas kernels  256 us (98%)
  local copies, waits for them, and re-layouts  5.31 us (2%)
    pallas_call x1, Pallas kernels, body_fn(): pl.pallas_call(lambda *refs: kernel(elem_count, *refs), out_shape=(jax.Sh...  256 us

profile of v4, /device:TPU:1, one launch (start us, length us, event | category | flops | bytes accessed | tf_op | source)
XLA Modules:
  0.0 261.6 jit_solution(15726430316294510677)
XLA Ops:
  0.6 1.8 copy.8
  2.4 255.6 %shard_map.67 = (f32[7,16,8,256]{3,2,1,0:T(8,128)}, f32[16,128]{1,0:T(8,128)}) custom-call(f32[512,4,4,512]{3,2,1,0:T(4,128)} %refs_0_.1, bf16[64,512,512]{2,1,0:T(8,128)(2,1)} %refs_1_.1, bf16[512,512]{1,0:T(8,128)(2,1)} %bitcast.7, bf16[1024,16]{1,0:T(8,128)(2,1)} %bitcast.5), custom_call_target="tpu_custom_call" | custom-call | tf_op jit(solution)/shard_map/pallas_call | solution.py:431
  258.0 1.3 slice_reduce_fusion
  259.4 2.2 copy.10

commit v5 on v4

v5 whole, which is shorter than its diff:
```python
import jax
import jax.numpy as jnp
from jax import lax
from jax.experimental import pallas as pl
from jax.experimental.pallas import tpu as pltpu
from jax.sharding import PartitionSpec as P

STEPS = 6
F32 = jnp.float32
BF16 = jnp.bfloat16
MESH = pl.DeviceIdType.MESH
NT = 64
BOND = 512
SLICE = 128
BLK = 16
QB = 256


def total(x):
    return jnp.sum(jnp.sum(x, axis=1, keepdims=True), axis=0, keepdims=True)


def blk(i, size):
    return pl.ds(pl.multiple_of(i * size, size), size)


def col_sum(x):
    return jnp.sum(x, axis=0, keepdims=True)


def sq_block(blk):
    out = jnp.zeros((8, SLICE), F32)
    sq = (blk * blk).reshape(BLK, 8, BOND).sum(axis=0)
    for i in range(4):
        out = out + sq[:, i * SLICE:(i + 1) * SLICE]
    return out


def kernel(elem_count, wave_ref, left_ref, right_ref, two_ref, kr_ref, ab_ref,
           slab, nslab, tmp, wide, ut, u_ref, rin, rb, lb, wt, y_ref, z_ref, acc, recv_s, recv_x, vecs, kbuf, wg, vg,
           red_n, red_a, red_b,
           ld_sem, sl_sem, r_send, r_recv, n_send, n_recv, s_send, s_recv, x_send, x_recv, a_send, a_recv,
           b_send, b_recv, g1_send, g1_recv, g2_send, g2_recv, g3_send, g3_recv, k_send, k_recv):
    r = lax.axis_index('rows')
    c = lax.axis_index('terms')
    x = lax.rem(r, 4)
    y = lax.rem(r // 4, 4)
    z = r // BLK
    g = r // 4
    row_base = r - x
    z_peers = [lax.rem(z + d, 4) * BLK + y * 4 + x for d in (1, 2, 3)]
    y_peers = [z * BLK + lax.rem(y + d, 4) * 4 + x for d in (1, 2, 3)]
    x_peers = [row_base + lax.rem(x + d, 4) for d in (1, 2, 3)]

    def pair(i, h):
        return pl.ds(8 * h + 2 * i, 2)

    def rcopy(src, dst, ssem, rsem, row, core):
        return pltpu.make_async_remote_copy(src_ref=src, dst_ref=dst, send_sem=ssem, recv_sem=rsem,
                                            device_id=(row, core), device_id_type=MESH)

    me = x * 2 + c
    group = [(row_base + lax.rem(me + d, 8) // 2, lax.rem(me + d, 2)) for d in range(1, 8)]
    plane = [(lax.rem(g + d, BLK) * 4 + x, c) for d in range(1, BLK)]
    barrier = pltpu.get_barrier_semaphore()
    for peer in group + plane:
        pl.semaphore_signal(barrier, inc=1, device_id=peer, device_id_type=MESH)

    cp_r = pltpu.make_async_copy(right_ref, rin.at[x], ld_sem.at[0])
    cp_r.start()
    n_loads, s_loads = [], []
    for p in range(BLK):
        rows_n = blk(z, SLICE)
        n_loads.append(pltpu.make_async_copy(wave_ref.at[rows_n, p // 4, p % 4, :], nslab.at[p], sl_sem.at[0, p]))
    for p in range(BLK):
        rows_s = blk(x, SLICE)
        s_loads.append(pltpu.make_async_copy(wave_ref.at[rows_s, p // 4, p % 4, :], slab.at[p], sl_sem.at[1, p]))
    cp_l = pltpu.make_async_copy(left_ref.at[:, blk(x, SLICE), :], lb, ld_sem.at[1])
    for cp in n_loads + s_loads:
        cp.start()
    cp_l.start()
    cp_r.wait()
    pl.semaphore_wait(barrier, len(group) + len(plane))

    right = row_base + lax.rem(x + 1, 4)
    left = row_base + lax.rem(x + 3, 4)
    xl = lax.rem(x + 3, 4)
    xr = lax.rem(x + 1, 4)
    halves = [pl.ds(0, QB), pl.ds(QB, QB)]

    def r_move(i, block, half, row):
        ref = rin.at[block, halves[half], :]
        return rcopy(ref, ref, r_send.at[i], r_recv.at[i], row, c)

    r0 = r_move(0, x, 0, right)
    r1 = r_move(1, x, 1, left)
    r2 = r_move(2, x, 1, right)
    r3 = r_move(3, x, 0, left)
    r4 = r_move(4, xl, 0, right)
    r5 = r_move(5, xr, 1, left)
    for cp in (r0, r1, r2, r3):
        cp.start()

    for cp in n_loads:
        cp.wait()

    ssq = jnp.zeros((8, SLICE), F32)
    ssq = lax.fori_loop(0, BLK, lambda p, acc: acc + sq_block(nslab[p]), ssq)
    red_n[0] = jnp.zeros((8, SLICE), F32) + total(ssq)
    n_copies = []
    for d, row in enumerate(z_peers):
        cp = rcopy(red_n.at[0], red_n.at[d + 1], n_send.at[d], n_recv.at[d], row, c)
        cp.start()
        n_copies.append(cp)

    lane16 = lax.broadcasted_iota(jnp.int32, (BLK, QB), 1)
    row16 = lax.broadcasted_iota(jnp.int32, (BLK, QB), 0)
    e_col = (lane16 // BLK == row16).astype(BF16)
    row_e = lax.broadcasted_iota(jnp.int32, (QB, BLK), 0)
    lane_e = lax.broadcasted_iota(jnp.int32, (QB, BLK), 1)
    e_row = (row_e // BLK == lane_e).astype(BF16)
    row_m = lax.broadcasted_iota(jnp.int32, (QB, QB), 0)
    lane_m = lax.broadcasted_iota(jnp.int32, (QB, QB), 1)
    diag = lax.rem(row_m, BLK) == lax.rem(lane_m, BLK)

    wide[...] = jnp.dot(two_ref[...], e_col, preferred_element_type=F32).astype(BF16)

    def build_w(kk, carry):
        for i in range(8):
            k = kk * 8 + i
            rows = wide[blk(k, BLK), :]
            full = jnp.dot(e_row, rows, preferred_element_type=F32)
            wt[k] = jnp.where(diag, full, 0.0).astype(BF16)
        return carry

    lax.fori_loop(0, NT // 8, build_w, 0)
    r0.wait_recv()
    r4.start()
    r1.wait_recv()
    r5.start()

    for cp in n_copies:
        cp.wait()
    norm = [red_n[lax.rem(z - s + 4, 4)] for s in range(4)]
    scale = jnp.sqrt(((norm[0] + norm[1]) + (norm[2] + norm[3]))[:1, :1] / elem_count)
    for cp in s_loads:
        cp.wait()
    vg[1] = jnp.zeros_like(vg[1])

    def first(p, carry):
        ut[p] = (slab[p] / scale).astype(BF16)
        ut[p + 8] = (slab[p + 8] / scale).astype(BF16)
        for n in range(4):
            tmp[n] = jnp.transpose(slab[p, :, n * SLICE:(n + 1) * SLICE])
        tmp[4] = jnp.transpose(slab[p + 8, :, blk(z, SLICE)])
        for n in range(4):
            vg[0, 0, n, blk(p, BLK), :] = tmp[n, blk(y * 2 + c, BLK), :] / scale
            vg[0, 1, n, blk(p, BLK), :] = tmp[4, blk(n * 2 + c, BLK), :] / scale
        return carry

    lax.fori_loop(0, 8, first, 0)
    vecs[0, :SLICE] = vg[0, 0, z]
    vecs[0, SLICE:] = vg[0, 1, y]

    out_lanes = blk(lax.rem(x, 2), SLICE)

    def piece(jv, h):
        return vecs.at[jv].reshape(BLK, BLK, SLICE).at[:, h * 8:(h + 1) * 8, :]

    def emit(jv):
        for h in range(2):
            dst_x = 2 * c + h
            dst_c = x // 2
            is_me = jnp.logical_and(dst_x == x, dst_c == c)

            @pl.when(jnp.logical_not(is_me))
            def _():
                rcopy(piece(jv, h), kbuf.at[jv, :, :, out_lanes], k_send.at[jv, h], k_recv.at[jv, lax.rem(x, 2)],
                      row_base + dst_x, dst_c).start()

            @pl.when(is_me)
            def _():
                kbuf[jv, :, :, out_lanes] = vecs[jv].reshape(BLK, BLK, SLICE)[:, h * 8:(h + 1) * 8, :]

    def build_r(bhi):
        def body(i, carry):
            rows = blk(i, 64)
            lo = rin[2 * bhi, rows, :].astype(F32).reshape(8, 8, BOND)
            hi = rin[2 * bhi + 1, rows, :].astype(F32).reshape(8, 8, BOND)
            both = jnp.concatenate([lo, hi], axis=1).reshape(SLICE, BOND)
            rb[bhi, blk(i, SLICE), :] = both.astype(BF16)
            return carry

        lax.fori_loop(0, 8, body, 0)

    def put_y(o, bhi, mc, pp):
        o = o.astype(BF16).reshape(32, BLK, QB)
        rows = pl.ds(mc * 32, 32)
        y_ref[rows, bhi, 2 * pp] = o[:, :, :SLICE]
        y_ref[rows, bhi, 2 * pp + 1] = o[:, :, SLICE:]

    def s1_first(bhi):
        def body(i, carry):
            for pp in (i, i + 4):
                w = ut[pl.ds(2 * pp, 2)].reshape(QB, BOND)
                for mc in range(2):
                    rows = rb[bhi, pl.ds(mc * BOND, BOND), :]
                    o = lax.dot_general(rows, w, (((1,), (1,)), ((), ())), preferred_element_type=F32)
                    put_y(o, bhi, mc, pp)
            return carry

        lax.fori_loop(0, 4, body, 0)

    def s1(pp):
        w = jnp.concatenate([u_ref[2 * pp + i].reshape(BOND, SLICE) for i in range(2)], axis=1)
        for bhi in range(2):
            for mc in range(2):
                put_y(jnp.dot(rb[bhi, pl.ds(mc * BOND, BOND), :], w, preferred_element_type=F32), bhi, mc, pp)

    for cp in (r2, r3):
        cp.wait_recv()
    emit(0)
    own = x // 2
    build_r(own)
    s1_first(own)
    for cp in (r4, r5):
        cp.wait_recv()
    build_r(1 - own)
    s1_first(1 - own)
    for cp in (r0, r1, r2, r3, r4, r5):
        cp.wait_send()
    cp_l.wait()

    row_id = lax.broadcasted_iota(jnp.int32, (8, SLICE), 0)
    ab_ref[...] = jnp.zeros_like(ab_ref)

    def pack(p, n, am, rr, ss):
        out = jnp.where(row_id == 0, p, 0.0)
        out = jnp.where(row_id == 1, n, out)
        out = jnp.where(row_id == 2, am, out)
        out = jnp.where(row_id == 3, rr, out)
        return jnp.where(row_id == 4, ss, out)

    def safe_div(num, den):
        ok = den > 0.0
        return jnp.where(ok, num / jnp.where(ok, den, 1.0), 0.0)

    def merge(p, n, am, rr, ss):
        n_all = col_sum(n)
        mean = safe_div(col_sum(am * n), n_all)
        gap = mean - am
        r_all = col_sum(rr + gap * (gap * n - 2.0 * ss))
        return col_sum(p), n_all, mean, r_all, col_sum(ss)

    def step(j, prev_beta):
        def s2(kk, carry):
            for i in range(BLK):
                k = kk * BLK + i
                rhs = jnp.concatenate([y_ref[k, 0].reshape(QB, SLICE), y_ref[k, 1].reshape(QB, SLICE)], axis=1)
                o = jnp.dot(wt[k], rhs, preferred_element_type=F32).astype(BF16)
                z_ref[0, k] = o[:, :SLICE]
                z_ref[1, k] = o[:, SLICE:]
            return carry

        lax.fori_loop(0, NT // BLK, s2, 0)


        order = [lax.rem(x + d, 4) for d in (2, 1, 3, 0)]

        def s3(bhi, out, lo):
            slices = [blk(pos, SLICE) for pos in order[lo:lo + 2]]
            outs = [None, None]
            for k0 in range(0, NT // 2, 8):
                for kh in range(2):
                    ks = k0 + kh * NT // 2
                    rhs = jnp.concatenate([lb[pl.ds(ks, 8), :, sl].reshape(1024, SLICE) for sl in slices], axis=1)
                    lhs = jnp.concatenate([z_ref[bhi, ks + k] for k in range(8)], axis=1)
                    o = jnp.dot(lhs, rhs, preferred_element_type=F32)
                    outs[kh] = o if outs[kh] is None else outs[kh] + o
            for n in range(2):
                cols = slice(n * SLICE, (n + 1) * SLICE)
                out[lo + n] = outs[0][:, cols] - (0.0 - outs[1][:, cols])

        acc_o = acc.at[1 - c]
        acc_m = acc.at[c]
        s_copies = []
        for n in range(2):
            two = pl.ds(2 * n, 2)
            s_copies.append(rcopy(acc_o.at[two], recv_s.at[two], s_send.at[n], s_recv.at[n], r, 1 - c))
        x_copies = []
        for n in range(3):
            x_copies.append(rcopy(acc_m.at[n], recv_x.at[n], x_send.at[n], x_recv.at[n], row_base + order[n], c))
        s3(1 - c, acc_o, 0)
        s_copies[0].start()
        s3(c, acc_m, 0)
        s_copies[0].wait_recv()
        for n in range(2):
            acc_m[n] += recv_s[n]
            x_copies[n].start()
        s3(1 - c, acc_o, 2)
        s_copies[1].start()
        s3(c, acc_m, 2)
        s_copies[1].wait_recv()
        acc_m[2] += recv_s[2]
        x_copies[2].start()
        w_own = acc_m[3] + recv_s[3]
        for cp in s_copies:
            cp.wait_send()
        for cp in x_copies:
            cp.wait()
        w_vec = (w_own + recv_x[0]) + (recv_x[1] + recv_x[2])
        v_cur = vecs[j]
        v_old = vecs[lax.max(j - 1, 0)]

        w_res = w_vec - prev_beta * v_old
        n_loc = total(v_cur * v_cur)
        a_loc = safe_div(total(w_res * v_cur), n_loc)
        e_loc = w_res - a_loc * v_cur
        red_a[0] = pack(total(w_vec * v_cur), n_loc, a_loc, total(e_loc * e_loc), total(e_loc * v_cur))

        a_copies = [rcopy(red_a.at[0], red_a.at[d + 1], a_send.at[d], a_recv.at[d], *peer) for d, peer in enumerate(group)]
        for cp in a_copies:
            cp.start()

        wg[0, z] = w_vec[:SLICE]
        wg[1, y] = w_vec[SLICE:]
        near = []
        for d in range(3):
            near.append(rcopy(wg.at[0, z], wg.at[0, z], g1_send.at[0, d], g1_recv.at[0, d], z_peers[d], c))
            near.append(rcopy(wg.at[1, y], wg.at[1, y], g1_send.at[1, d], g1_recv.at[1, d], y_peers[d], c))

        @pl.when(j < STEPS - 1)
        def _():
            for cp in near:
                cp.start()

        for cp in a_copies:
            cp.wait()
        blocks = [red_a[lax.rem(me - s + 8, 8)] for s in range(8)]

        def gather_rows(blks, i):
            return jnp.concatenate([bk[i:i + 1, :] for bk in blks], axis=0)

        par = lax.rem(j, 2)
        red_b[par, 0] = pack(*merge(*[gather_rows(blocks, i) for i in range(5)]))
        b_copies = []
        for d, peer in enumerate(plane):
            b_copies.append(rcopy(red_b.at[par, 0], red_b.at[par, d + 1], b_send.at[par, d], b_recv.at[par, d], *peer))
        for cp in b_copies:
            cp.start()
        for cp in b_copies:
            cp.wait()
        blocks = [red_b[par, lax.rem(g - s + BLK, BLK)] for s in range(BLK)]
        p_all, n_all, a_all, r_all, s_all = [gather_rows(blocks, i) for i in range(5)]
        alpha = col_sum(p_all) / elem_count
        gap = alpha - a_all
        beta = jnp.sqrt(col_sum(r_all + gap * (gap * n_all - 2.0 * s_all)) / elem_count)
        alpha_s = alpha[:, :1]
        beta_s = beta[:, :1]

        v_new = (w_vec - alpha_s * v_cur - prev_beta * v_old) / beta_s
        vecs[j + 1] = v_new
        ab_ref[pl.ds(j, 1), :] = alpha
        ab_ref[pl.ds(8 + j, 1), :] = beta

        emit(j + 1)

        @pl.when(j < STEPS - 1)
        def _():
            for cp in near:
                cp.wait()
            new = lax.rem(j + 1, 2)
            for h in range(2):
                for n in range(4):
                    v = (wg[h, n] - alpha_s * vg[1 - new, h, n] - prev_beta * vg[new, h, n]) / beta_s
                    vg[new, h, n] = v
                    at = (z, n) if h else (n, y)
                    u_ref[pl.ds(8 * h, 8), at[0], at[1], c] = v.astype(BF16).reshape(8, BLK, SLICE)
            moves = [(h, d) for h in range(2) for d in range(3)]
            cuts = range(4)

            def move(sems, h, i, d, ref, across):
                row = z_peers[d] if across else y_peers[d]
                return rcopy(ref, ref, sems[0].at[h, i, d], sems[1].at[h, i, d], row, c)

            def p2(i, h, d):
                ref = u_ref.at[pair(i, h), z, :, c] if h else u_ref.at[pair(i, h), :, y, c]
                return move((g2_send, g2_recv), h, i, d, ref, h == 1)

            def p3(i, h):
                ref = u_ref.at[pair(i, h), :, :, c]
                return rcopy(ref, ref, g3_send.at[h, i], g3_recv.at[h, i], r, 1 - c)

            def product(i):
                for h in range(2):
                    p3(i, h).wait_recv()
                s1(i)
                s1(4 + i)

            for i in cuts:
                for h, d in moves:
                    p2(i, h, d).start()
            for i in cuts:
                for h, d in moves:
                    p2(i, h, d).wait_recv()
                for h in range(2):
                    p3(i, h).start()
                if i:
                    product(i - 1)
            product(cuts[-1])
            for i in cuts:
                for h, d in moves:
                    p2(i, h, d).wait_send()
                for h in range(2):
                    p3(i, h).wait_send()

        return beta_s

    lax.fori_loop(0, STEPS, step, jnp.zeros((1, 1), F32))

    def drain(jv, carry):
        for h in range(2):
            dst_x = 2 * c + h
            dst_c = x // 2

            @pl.when(jnp.logical_not(jnp.logical_and(dst_x == x, dst_c == c)))
            def _():
                rcopy(piece(jv, h), kbuf.at[jv, :, :, 0:SLICE], k_send.at[jv, h], k_recv.at[jv, 0],
                      row_base + dst_x, dst_c).wait_send()

        for m in range(2):
            src_x = 2 * c + m
            src_c = x // 2

            @pl.when(jnp.logical_not(jnp.logical_and(src_x == x, src_c == c)))
            def _():
                rcopy(piece(jv, 0), kbuf.at[jv, :, :, m * SLICE:(m + 1) * SLICE], k_send.at[jv, 0], k_recv.at[jv, m],
                      row_base + src_x, src_c).wait_recv()

        return carry

    lax.fori_loop(0, STEPS + 1, drain, 0)
    cp_k = pltpu.make_async_copy(kbuf, kr_ref, ld_sem.at[0])
    cp_k.start()
    cp_k.wait()


def solution(mesh):
    assert mesh.shape['terms'] == 2 and mesh.shape['rows'] == 64

    def body_fn(wavefunc, left_loc, two_loc, right_loc):
        elem_count = float(wavefunc.size)
        vm = pl.BlockSpec(memory_space=pltpu.VMEM)
        hbm = pl.BlockSpec(memory_space=pl.ANY)
        dma = pltpu.SemaphoreType.DMA
        kr, ab = pl.pallas_call(
            lambda *refs: kernel(elem_count, *refs),
            out_shape=(jax.ShapeDtypeStruct((STEPS + 1, BLK, 8, QB), F32), jax.ShapeDtypeStruct((BLK, SLICE), F32)),
            in_specs=[hbm, hbm, hbm, vm],
            out_specs=(hbm, vm),
            scratch_shapes=[
                pltpu.VMEM((BLK, SLICE, BOND), F32),
                pltpu.VMEM((BLK, SLICE, BOND), F32),
                pltpu.VMEM((5, SLICE, SLICE), F32),
                pltpu.VMEM((1024, QB), BF16),
                pltpu.VMEM((BLK, SLICE, BOND), BF16),
                pltpu.VMEM((BLK, 4, 4, 2, BLK, SLICE), BF16),
                pltpu.VMEM((4, BOND, BOND), BF16),
                pltpu.VMEM((2, 1024, BOND), BF16),
                pltpu.VMEM((NT, SLICE, BOND), BF16),
                pltpu.VMEM((NT, QB, QB), BF16),
                pltpu.VMEM((NT, 2, BLK, BLK, SLICE), BF16),
                pltpu.VMEM((2, NT, QB, SLICE), BF16),
                pltpu.VMEM((2, 4, QB, SLICE), F32),
                pltpu.VMEM((4, QB, SLICE), F32),
                pltpu.VMEM((3, QB, SLICE), F32),
                pltpu.VMEM((STEPS + 1, QB, SLICE), F32),
                pltpu.VMEM((STEPS + 1, BLK, 8, QB), F32),
                pltpu.VMEM((2, 4, SLICE, SLICE), F32),
                pltpu.VMEM((2, 2, 4, SLICE, SLICE), F32),
                pltpu.VMEM((4, 8, SLICE), F32),
                pltpu.VMEM((8, 8, SLICE), F32),
                pltpu.VMEM((2, BLK, 8, SLICE), F32),
                dma((2,)), dma((2, BLK)), dma((6,)), dma((6,)), dma((3,)), dma((3,)), dma((2,)), dma((2,)), dma((3,)), dma((3,)),
                dma((7,)), dma((7,)), dma((2, 15)), dma((2, 15)),
                dma((2, 3)), dma((2, 3)), dma((2, 4, 3)), dma((2, 4, 3)), dma((2, 4)), dma((2, 4)),
                dma((STEPS + 1, 2)), dma((STEPS + 1, 2)),
            ],
            compiler_params=pltpu.CompilerParams(has_side_effects=True, collective_id=0, vmem_limit_bytes=60 * 1024 * 1024),
        )(wavefunc, left_loc, right_loc.reshape(BOND, BOND), two_loc.reshape(1024, BLK))
        krylov = jnp.transpose(kr.reshape(STEPS + 1, 4, 4, 8, QB), (0, 4, 1, 2, 3))
        return krylov, ab[:STEPS, 0], ab[8:8 + STEPS, 0]

    return jax.shard_map(body_fn, mesh=mesh, in_specs=(P(), P('terms'), P('terms'), P('terms', 'rows')),
                         out_specs=(P(None, 'terms', None, None, 'rows'), P(), P()), check_vma=False)
```

time: 262 us -> 241 us (0.920)
  Pallas kernels: 256 us -> 235 us
    pallas_call x1, Pallas kernels: 256 us -> 235 us  [body_fn(): pl.pallas_call(lambda *refs: kernel(elem_count, *refs), out_shape=(jax.Sh...]
where the time goes in v5:
time: 241 us
  Pallas kernels  235 us (98%)
  local copies, waits for them, and re-layouts  5.31 us (2%)
    pallas_call x1, Pallas kernels, body_fn(): pl.pallas_call(lambda *refs: kernel(elem_count, *refs), out_shape=(jax.Sh...  235 us

profile of v5, /device:TPU:1, one launch (start us, length us, event | category | flops | bytes accessed | tf_op | source)
XLA Modules:
  0.0 240.5 jit_solution(10688564425078470083)
XLA Ops:
  0.6 1.8 copy.8
  2.4 234.6 %shard_map.67 = (f32[7,16,8,256]{3,2,1,0:T(8,128)}, f32[16,128]{1,0:T(8,128)}) custom-call(f32[512,4,4,512]{3,2,1,0:T(4,128)} %refs_0_.1, bf16[64,512,512]{2,1,0:T(8,128)(2,1)} %refs_1_.1, bf16[512,512]{1,0:T(8,128)(2,1)} %bitcast.7, bf16[1024,16]{1,0:T(8,128)(2,1)} %bitcast.5), custom_call_target="tpu_custom_call" | custom-call | tf_op jit(solution)/shard_map/pallas_call | solution.py:456
  237.0 1.3 slice_reduce_fusion
  238.3 2.2 copy.10

commit v6 on v5

--- a/solution.py
+++ b/solution.py
@@ -37,10 +37,10 @@
 
 
 def kernel(elem_count, wave_ref, left_ref, right_ref, two_ref, kr_ref, ab_ref,
-           slab, nslab, tmp, wide, ut, u_ref, rin, rb, lb, wt, y_ref, z_ref, acc, recv_s, recv_x, vecs, kbuf, wg, vg,
+           slab, nslab, tmp, wide, ut, u_ref, rin, rb, lb, wt, y_ref, z_ref, acc, recv_s, recv_x, vecs, kbuf, wg, vg, wq, vq,
            red_n, red_a, red_b,
            ld_sem, sl_sem, r_send, r_recv, n_send, n_recv, s_send, s_recv, x_send, x_recv, a_send, a_recv,
-           b_send, b_recv, g1_send, g1_recv, g2_send, g2_recv, g3_send, g3_recv, k_send, k_recv):
+           b_send, b_recv, g1_send, g1_recv, f_send, f_recv, g2_send, g2_recv, g3_send, g3_recv, k_send, k_recv):
     r = lax.axis_index('rows')
     c = lax.axis_index('terms')
     x = lax.rem(r, 4)
@@ -159,6 +159,19 @@
         return carry
 
     lax.fori_loop(0, 8, first, 0)
+    vq[1] = jnp.zeros_like(vq[1])
+
+    def first_pairs(p, carry):
+        for h in range(2):
+            for n in range(4):
+                tmp[n] = jnp.transpose(slab[8 * h + p, :, n * SLICE:(n + 1) * SLICE])
+            for n in range(4):
+                for m in range(4):
+                    at = (n, m) if h else (m, n)
+                    vq[0, h, at[0], at[1], blk(p, BLK), :] = tmp[n, blk(m * 2 + c, BLK), :] / scale
+        return carry
+
+    lax.fori_loop(0, 2, first_pairs, 0)
     vecs[0, :SLICE] = vg[0, 0, z]
     vecs[0, SLICE:] = vg[0, 1, y]
 
@@ -253,16 +266,11 @@
         return col_sum(p), n_all, mean, r_all, col_sum(ss)
 
     def step(j, prev_beta):
-        def s2(kk, carry):
-            for i in range(BLK):
-                k = kk * BLK + i
-                rhs = jnp.concatenate([y_ref[k, 0].reshape(QB, SLICE), y_ref[k, 1].reshape(QB, SLICE)], axis=1)
-                o = jnp.dot(wt[k], rhs, preferred_element_type=F32).astype(BF16)
-                z_ref[0, k] = o[:, :SLICE]
-                z_ref[1, k] = o[:, SLICE:]
-            return carry
-
-        lax.fori_loop(0, NT // BLK, s2, 0)
+        for k in range(NT):
+            rhs = jnp.concatenate([y_ref[k, bhi].reshape(QB, SLICE) for bhi in range(2)], axis=1)
+            o = jnp.dot(wt[k], rhs, preferred_element_type=F32).astype(BF16)
+            z_ref[0, k] = o[:, :SLICE]
+            z_ref[1, k] = o[:, SLICE:]
 
 
         order = [lax.rem(x + d, 4) for d in (2, 1, 3, 0)]
@@ -348,6 +356,21 @@
             b_copies.append(rcopy(red_b.at[par, 0], red_b.at[par, d + 1], b_send.at[par, d], b_recv.at[par, d], *peer))
         for cp in b_copies:
             cp.start()
+
+        far = []
+        for d in range(3):
+            far.append(rcopy(wq.at[0, y], wq.at[0, y], f_send.at[0, d], f_recv.at[0, d], y_peers[d], c))
+            far.append(rcopy(wq.at[1, z], wq.at[1, z], f_send.at[1, d], f_recv.at[1, d], z_peers[d], c))
+
+        @pl.when(j < STEPS - 1)
+        def _():
+            for cp in near:
+                cp.wait()
+            wq[0, y] = wg[0, :, :32]
+            wq[1, z] = wg[1, :, :32]
+            for cp in far:
+                cp.start()
+
         for cp in b_copies:
             cp.wait()
         blocks = [red_b[par, lax.rem(g - s + BLK, BLK)] for s in range(BLK)]
@@ -367,8 +390,6 @@
 
         @pl.when(j < STEPS - 1)
         def _():
-            for cp in near:
-                cp.wait()
             new = lax.rem(j + 1, 2)
             for h in range(2):
                 for n in range(4):
@@ -397,20 +418,31 @@
                 s1(i)
                 s1(4 + i)
 
-            for i in cuts:
+            for i in cuts[1:]:
                 for h, d in moves:
                     p2(i, h, d).start()
+            for cp in far:
+                cp.wait()
+            for h in range(2):
+                for m in range(4):
+                    v = (wq[h, m] - alpha_s * vq[1 - new, h, m] - prev_beta * vq[new, h, m]) / beta_s
+                    vq[new, h, m] = v
+                    for n in range(4):
+                        at = (m, n) if h else (n, m)
+                        u_ref[pair(0, h), at[0], at[1], c] = v[n].astype(BF16).reshape(2, BLK, SLICE)
             for i in cuts:
-                for h, d in moves:
-                    p2(i, h, d).wait_recv()
+                if i:
+                    for h, d in moves:
+                        p2(i, h, d).wait_recv()
                 for h in range(2):
                     p3(i, h).start()
                 if i:
                     product(i - 1)
             product(cuts[-1])
             for i in cuts:
-                for h, d in moves:
-                    p2(i, h, d).wait_send()
+                if i:
+                    for h, d in moves:
+                        p2(i, h, d).wait_send()
                 for h in range(2):
                     p3(i, h).wait_send()
 
@@ -478,12 +510,14 @@
                 pltpu.VMEM((STEPS + 1, BLK, 8, QB), F32),
                 pltpu.VMEM((2, 4, SLICE, SLICE), F32),
                 pltpu.VMEM((2, 2, 4, SLICE, SLICE), F32),
+                pltpu.VMEM((2, 4, 4, 32, SLICE), F32),
+                pltpu.VMEM((2, 2, 4, 4, 32, SLICE), F32),
                 pltpu.VMEM((4, 8, SLICE), F32),
                 pltpu.VMEM((8, 8, SLICE), F32),
                 pltpu.VMEM((2, BLK, 8, SLICE), F32),
                 dma((2,)), dma((2, BLK)), dma((6,)), dma((6,)), dma((3,)), dma((3,)), dma((2,)), dma((2,)), dma((3,)), dma((3,)),
                 dma((7,)), dma((7,)), dma((2, 15)), dma((2, 15)),
-                dma((2, 3)), dma((2, 3)), dma((2, 4, 3)), dma((2, 4, 3)), dma((2, 4)), dma((2, 4)),
+                dma((2, 3)), dma((2, 3)), dma((2, 3)), dma((2, 3)), dma((2, 4, 3)), dma((2, 4, 3)), dma((2, 4)), dma((2, 4)),
                 dma((STEPS + 1, 2)), dma((STEPS + 1, 2)),
             ],
             compiler_params=pltpu.CompilerParams(has_side_effects=True, collective_id=0, vmem_limit_bytes=60 * 1024 * 1024),

time: 241 us -> 231 us (0.959)
  Pallas kernels: 235 us -> 224 us
    pallas_call x1, Pallas kernels: 235 us -> 224 us  [body_fn(): pl.pallas_call(lambda *refs: kernel(elem_count, *refs), out_shape=(jax.Sh...]
where the time goes in v6:
time: 231 us; the launch traced here: 230 us
  Pallas kernels  224 us (97%)
  local copies, waits for them, and re-layouts  5.31 us (2%)
    pallas_call x1, Pallas kernels, body_fn(): pl.pallas_call(lambda *refs: kernel(elem_count, *refs), out_shape=(jax.Sh...  224 us

profile of v6, /device:TPU:1, one launch (start us, length us, event | category | flops | bytes accessed | tf_op | source)
XLA Modules:
  0.0 230.4 jit_solution(2059233776288668730)
XLA Ops:
  0.6 1.8 copy.8
  2.4 224.4 %shard_map.67 = (f32[7,16,8,256]{3,2,1,0:T(8,128)}, f32[16,128]{1,0:T(8,128)}) custom-call(f32[512,4,4,512]{3,2,1,0:T(4,128)} %refs_0_.1, bf16[64,512,512]{2,1,0:T(8,128)(2,1)} %refs_1_.1, bf16[512,512]{1,0:T(8,128)(2,1)} %bitcast.7, bf16[1024,16]{1,0:T(8,128)(2,1)} %bitcast.5), custom_call_target="tpu_custom_call" | custom-call | tf_op jit(solution)/shard_map/pallas_call | solution.py:488
  226.9 1.3 slice_reduce_fusion
  228.2 2.2 copy.10

commit v7 on v6

--- a/solution.py
+++ b/solution.py
@@ -88,16 +88,18 @@
     xr = lax.rem(x + 1, 4)
     halves = [pl.ds(0, QB), pl.ds(QB, QB)]
 
-    def r_move(i, block, half, row):
-        ref = rin.at[block, halves[half], :]
+    quarters = [pl.ds(i * SLICE, SLICE) for i in range(4)]
+
+    def r_move(i, block, rows, row):
+        ref = rin.at[block, rows, :]
         return rcopy(ref, ref, r_send.at[i], r_recv.at[i], row, c)
 
-    r0 = r_move(0, x, 0, right)
-    r1 = r_move(1, x, 1, left)
-    r2 = r_move(2, x, 1, right)
-    r3 = r_move(3, x, 0, left)
-    r4 = r_move(4, xl, 0, right)
-    r5 = r_move(5, xr, 1, left)
+    r0 = r_move(0, x, halves[0], right)
+    r1 = r_move(1, x, halves[1], left)
+    r2 = r_move(2, x, halves[1], right)
+    r3 = r_move(3, x, halves[0], left)
+    r4 = [r_move(4 + i, xl, quarters[i], right) for i in range(2)]
+    r5 = [r_move(6 + i, xr, quarters[2 + i], left) for i in range(2)]
     for cp in (r0, r1, r2, r3):
         cp.start()
 
@@ -135,9 +137,11 @@
 
     lax.fori_loop(0, NT // 8, build_w, 0)
     r0.wait_recv()
-    r4.start()
+    for cp in r4:
+        cp.start()
     r1.wait_recv()
-    r5.start()
+    for cp in r5:
+        cp.start()
 
     for cp in n_copies:
         cp.wait()
@@ -195,31 +199,30 @@
             def _():
                 kbuf[jv, :, :, out_lanes] = vecs[jv].reshape(BLK, BLK, SLICE)[:, h * 8:(h + 1) * 8, :]
 
-    def build_r(bhi):
-        def body(i, carry):
-            rows = blk(i, 64)
-            lo = rin[2 * bhi, rows, :].astype(F32).reshape(8, 8, BOND)
-            hi = rin[2 * bhi + 1, rows, :].astype(F32).reshape(8, 8, BOND)
-            both = jnp.concatenate([lo, hi], axis=1).reshape(SLICE, BOND)
-            rb[bhi, blk(i, SLICE), :] = both.astype(BF16)
-            return carry
-
-        lax.fori_loop(0, 8, body, 0)
-
-    def put_y(o, bhi, mc, pp):
-        o = o.astype(BF16).reshape(32, BLK, QB)
-        rows = pl.ds(mc * 32, 32)
+    def build_r(bhi, parts):
+        for i in parts:
+            rows = quarters[i]
+            lo = rin[2 * bhi, rows, :].astype(F32).reshape(BLK, 8, BOND)
+            hi = rin[2 * bhi + 1, rows, :].astype(F32).reshape(BLK, 8, BOND)
+            both = jnp.concatenate([lo, hi], axis=1).reshape(QB, BOND)
+            rb[bhi, pl.ds(i * QB, QB), :] = both.astype(BF16)
+
+    def put_y(o, bhi, first_k, pp):
+        o = o.astype(BF16).reshape(-1, BLK, QB)
+        rows = pl.ds(first_k, o.shape[0])
         y_ref[rows, bhi, 2 * pp] = o[:, :, :SLICE]
         y_ref[rows, bhi, 2 * pp + 1] = o[:, :, SLICE:]
 
-    def s1_first(bhi):
+    def s1_first(bhi, parts):
+        build_r(bhi, parts)
+
         def body(i, carry):
             for pp in (i, i + 4):
                 w = ut[pl.ds(2 * pp, 2)].reshape(QB, BOND)
-                for mc in range(2):
-                    rows = rb[bhi, pl.ds(mc * BOND, BOND), :]
+                for m in parts:
+                    rows = rb[bhi, pl.ds(m * QB, QB), :]
                     o = lax.dot_general(rows, w, (((1,), (1,)), ((), ())), preferred_element_type=F32)
-                    put_y(o, bhi, mc, pp)
+                    put_y(o, bhi, m * BLK, pp)
             return carry
 
         lax.fori_loop(0, 4, body, 0)
@@ -228,19 +231,18 @@
         w = jnp.concatenate([u_ref[2 * pp + i].reshape(BOND, SLICE) for i in range(2)], axis=1)
         for bhi in range(2):
             for mc in range(2):
-                put_y(jnp.dot(rb[bhi, pl.ds(mc * BOND, BOND), :], w, preferred_element_type=F32), bhi, mc, pp)
+                put_y(jnp.dot(rb[bhi, pl.ds(mc * BOND, BOND), :], w, preferred_element_type=F32), bhi, mc * 32, pp)
 
     for cp in (r2, r3):
         cp.wait_recv()
     emit(0)
     own = x // 2
-    build_r(own)
-    s1_first(own)
-    for cp in (r4, r5):
-        cp.wait_recv()
-    build_r(1 - own)
-    s1_first(1 - own)
-    for cp in (r0, r1, r2, r3, r4, r5):
+    s1_first(own, range(4))
+    for i in range(2):
+        r4[i].wait_recv()
+        r5[i].wait_recv()
+        s1_first(1 - own, (i, 2 + i))
+    for cp in [r0, r1, r2, r3] + r4 + r5:
         cp.wait_send()
     cp_l.wait()
 
@@ -381,51 +383,53 @@
         alpha_s = alpha[:, :1]
         beta_s = beta[:, :1]
 
-        v_new = (w_vec - alpha_s * v_cur - prev_beta * v_old) / beta_s
+        def advance(w, cur, old):
+            return (w - alpha_s * cur - prev_beta * old) / beta_s
+
+        new = lax.rem(j + 1, 2)
+        moves = [(h, d) for h in range(2) for d in range(3)]
+        cuts = range(4)
+
+        def p2(i, h, d):
+            ref = u_ref.at[pair(i, h), z, :, c] if h else u_ref.at[pair(i, h), :, y, c]
+            row = z_peers[d] if h else y_peers[d]
+            return rcopy(ref, ref, g2_send.at[h, i, d], g2_recv.at[h, i, d], row, c)
+
+        def p3(i, h):
+            ref = u_ref.at[pair(i, h), :, :, c]
+            return rcopy(ref, ref, g3_send.at[h, i], g3_recv.at[h, i], r, 1 - c)
+
+        def product(i):
+            for h in range(2):
+                p3(i, h).wait_recv()
+            s1(i)
+            s1(4 + i)
+
+        @pl.when(j < STEPS - 1)
+        def _():
+            for i in cuts[1:]:
+                rows = pl.ds(32 * i, 32)
+                for h in range(2):
+                    for n in range(4):
+                        v = advance(wg[h, n, rows], vg[1 - new, h, n, rows], vg[new, h, n, rows])
+                        vg[new, h, n, rows] = v
+                        at = (z, n) if h else (n, y)
+                        u_ref[pair(i, h), at[0], at[1], c] = v.astype(BF16).reshape(2, BLK, SLICE)
+                for h, d in moves:
+                    p2(i, h, d).start()
+
+        v_new = advance(w_vec, v_cur, v_old)
         vecs[j + 1] = v_new
         ab_ref[pl.ds(j, 1), :] = alpha
         ab_ref[pl.ds(8 + j, 1), :] = beta
 
-        emit(j + 1)
-
         @pl.when(j < STEPS - 1)
         def _():
-            new = lax.rem(j + 1, 2)
-            for h in range(2):
-                for n in range(4):
-                    v = (wg[h, n] - alpha_s * vg[1 - new, h, n] - prev_beta * vg[new, h, n]) / beta_s
-                    vg[new, h, n] = v
-                    at = (z, n) if h else (n, y)
-                    u_ref[pl.ds(8 * h, 8), at[0], at[1], c] = v.astype(BF16).reshape(8, BLK, SLICE)
-            moves = [(h, d) for h in range(2) for d in range(3)]
-            cuts = range(4)
-
-            def move(sems, h, i, d, ref, across):
-                row = z_peers[d] if across else y_peers[d]
-                return rcopy(ref, ref, sems[0].at[h, i, d], sems[1].at[h, i, d], row, c)
-
-            def p2(i, h, d):
-                ref = u_ref.at[pair(i, h), z, :, c] if h else u_ref.at[pair(i, h), :, y, c]
-                return move((g2_send, g2_recv), h, i, d, ref, h == 1)
-
-            def p3(i, h):
-                ref = u_ref.at[pair(i, h), :, :, c]
-                return rcopy(ref, ref, g3_send.at[h, i], g3_recv.at[h, i], r, 1 - c)
-
-            def product(i):
-                for h in range(2):
-                    p3(i, h).wait_recv()
-                s1(i)
-                s1(4 + i)
-
-            for i in cuts[1:]:
-                for h, d in moves:
-                    p2(i, h, d).start()
             for cp in far:
                 cp.wait()
             for h in range(2):
                 for m in range(4):
-                    v = (wq[h, m] - alpha_s * vq[1 - new, h, m] - prev_beta * vq[new, h, m]) / beta_s
+                    v = advance(wq[h, m], vq[1 - new, h, m], vq[new, h, m])
                     vq[new, h, m] = v
                     for n in range(4):
                         at = (m, n) if h else (n, m)
@@ -446,6 +450,7 @@
                 for h in range(2):
                     p3(i, h).wait_send()
 
+        emit(j + 1)
         return beta_s
 
     lax.fori_loop(0, STEPS, step, jnp.zeros((1, 1), F32))
@@ -515,7 +520,7 @@
                 pltpu.VMEM((4, 8, SLICE), F32),
                 pltpu.VMEM((8, 8, SLICE), F32),
                 pltpu.VMEM((2, BLK, 8, SLICE), F32),
-                dma((2,)), dma((2, BLK)), dma((6,)), dma((6,)), dma((3,)), dma((3,)), dma((2,)), dma((2,)), dma((3,)), dma((3,)),
+                dma((2,)), dma((2, BLK)), dma((8,)), dma((8,)), dma((3,)), dma((3,)), dma((2,)), dma((2,)), dma((3,)), dma((3,)),
                 dma((7,)), dma((7,)), dma((2, 15)), dma((2, 15)),
                 dma((2, 3)), dma((2, 3)), dma((2, 3)), dma((2, 3)), dma((2, 4, 3)), dma((2, 4, 3)), dma((2, 4)), dma((2, 4)),
                 dma((STEPS + 1, 2)), dma((STEPS + 1, 2)),

time: 231 us -> 229 us (level)
  no operation moved by 1% of the time
where the time goes in v7:
time: 229 us
  Pallas kernels  223 us (97%)
  local copies, waits for them, and re-layouts  5.31 us (2%)
    pallas_call x1, Pallas kernels, body_fn(): pl.pallas_call(lambda *refs: kernel(elem_count, *refs), out_shape=(jax.Sh...  223 us

profile of v7, /device:TPU:1, one launch (start us, length us, event | category | flops | bytes accessed | tf_op | source)
XLA Modules:
  0.0 229.1 jit_solution(17970731889770976157)
XLA Ops:
  0.6 1.8 copy.8
  2.4 223.2 %shard_map.67 = (f32[7,16,8,256]{3,2,1,0:T(8,128)}, f32[16,128]{1,0:T(8,128)}) custom-call(f32[512,4,4,512]{3,2,1,0:T(4,128)} %refs_0_.1, bf16[64,512,512]{2,1,0:T(8,128)(2,1)} %refs_1_.1, bf16[512,512]{1,0:T(8,128)(2,1)} %bitcast.7, bf16[1024,16]{1,0:T(8,128)(2,1)} %bitcast.5), custom_call_target="tpu_custom_call" | custom-call | tf_op jit(solution)/shard_map/pallas_call | solution.py:493
  225.6 1.3 slice_reduce_fusion
  226.9 2.2 copy.10

commit v8 on v7

--- a/solution.py
+++ b/solution.py
@@ -115,9 +115,6 @@
         cp.start()
         n_copies.append(cp)
 
-    lane16 = lax.broadcasted_iota(jnp.int32, (BLK, QB), 1)
-    row16 = lax.broadcasted_iota(jnp.int32, (BLK, QB), 0)
-    e_col = (lane16 // BLK == row16).astype(BF16)
     row_e = lax.broadcasted_iota(jnp.int32, (QB, BLK), 0)
     lane_e = lax.broadcasted_iota(jnp.int32, (QB, BLK), 1)
     e_row = (row_e // BLK == lane_e).astype(BF16)
@@ -125,12 +122,15 @@
     lane_m = lax.broadcasted_iota(jnp.int32, (QB, QB), 1)
     diag = lax.rem(row_m, BLK) == lax.rem(lane_m, BLK)
 
-    wide[...] = jnp.dot(two_ref[...], e_col, preferred_element_type=F32).astype(BF16)
+    by_term = jnp.transpose(two_ref[...].astype(F32)).astype(BF16)
+    for q in range(BLK):
+        pick = (row_m == q * BLK + lane_m // BLK).astype(BF16)
+        wide[q] = jnp.dot(by_term, pick, preferred_element_type=F32)
 
     def build_w(kk, carry):
         for i in range(8):
             k = kk * 8 + i
-            rows = wide[blk(k, BLK), :]
+            rows = wide[:, k, :].astype(BF16)
             full = jnp.dot(e_row, rows, preferred_element_type=F32)
             wt[k] = jnp.where(diag, full, 0.0).astype(BF16)
         return carry
@@ -499,7 +499,7 @@
                 pltpu.VMEM((BLK, SLICE, BOND), F32),
                 pltpu.VMEM((BLK, SLICE, BOND), F32),
                 pltpu.VMEM((5, SLICE, SLICE), F32),
-                pltpu.VMEM((1024, QB), BF16),
+                pltpu.VMEM((BLK, NT, QB), F32),
                 pltpu.VMEM((BLK, SLICE, BOND), BF16),
                 pltpu.VMEM((BLK, 4, 4, 2, BLK, SLICE), BF16),
                 pltpu.VMEM((4, BOND, BOND), BF16),
@@ -526,7 +526,7 @@
                 dma((STEPS + 1, 2)), dma((STEPS + 1, 2)),
             ],
             compiler_params=pltpu.CompilerParams(has_side_effects=True, collective_id=0, vmem_limit_bytes=60 * 1024 * 1024),
-        )(wavefunc, left_loc, right_loc.reshape(BOND, BOND), two_loc.reshape(1024, BLK))
+        )(wavefunc, left_loc, right_loc.reshape(BOND, BOND), jnp.transpose(two_loc, (1, 2, 0)).reshape(QB, NT))
         krylov = jnp.transpose(kr.reshape(STEPS + 1, 4, 4, 8, QB), (0, 4, 1, 2, 3))
         return krylov, ab[:STEPS, 0], ab[8:8 + STEPS, 0]
 

time: 229 us -> 228 us (level)
  no operation moved by 1% of the time
where the time goes in v8:
time: 228 us
  Pallas kernels  224 us (98%)
  local copies, waits for them, and re-layouts  3.54 us (2%)
    pallas_call x1, Pallas kernels, body_fn(): pl.pallas_call(lambda *refs: kernel(elem_count, *refs), out_shape=(jax.Sh...  224 us

profile of v8, /device:TPU:1, one launch (start us, length us, event | category | flops | bytes accessed | tf_op | source)
XLA Modules:
  0.0 227.9 jit_solution(10278810975102173495)
XLA Ops:
  0.6 223.7 %shard_map.67 = (f32[7,16,8,256]{3,2,1,0:T(8,128)}, f32[16,128]{1,0:T(8,128)}) custom-call(f32[512,4,4,512]{3,2,1,0:T(4,128)} %refs_0_.1, bf16[64,512,512]{2,1,0:T(8,128)(2,1)} %refs_1_.1, bf16[512,512]{1,0:T(8,128)(2,1)} %bitcast.8, bf16[256,64]{1,0:T(8,128)(2,1)} %bitcast.9), custom_call_target="tpu_custom_call" | custom-call | tf_op jit(solution)/shard_map/pallas_call | solution.py:493
  224.3 1.3 slice_reduce_fusion
  225.7 2.2 copy.8

commit v9 on v8

--- a/solution.py
+++ b/solution.py
@@ -235,7 +235,6 @@
 
     for cp in (r2, r3):
         cp.wait_recv()
-    emit(0)
     own = x // 2
     s1_first(own, range(4))
     for i in range(2):
@@ -245,6 +244,7 @@
     for cp in [r0, r1, r2, r3] + r4 + r5:
         cp.wait_send()
     cp_l.wait()
+    emit(0)
 
     row_id = lax.broadcasted_iota(jnp.int32, (8, SLICE), 0)
     ab_ref[...] = jnp.zeros_like(ab_ref)

time: 228 us -> 226 us (level)
  Pallas kernels: 224 us -> 221 us
where the time goes in v9:
time: 226 us
  Pallas kernels  221 us (98%)
  local copies, waits for them, and re-layouts  3.54 us (2%)
    pallas_call x1, Pallas kernels, body_fn(): pl.pallas_call(lambda *refs: kernel(elem_count, *refs), out_shape=(jax.Sh...  221 us

profile of v9, /device:TPU:1, one launch (start us, length us, event | category | flops | bytes accessed | tf_op | source)
XLA Modules:
  0.0 225.7 jit_solution(2645625517111643010)
XLA Ops:
  0.6 221.5 %shard_map.67 = (f32[7,16,8,256]{3,2,1,0:T(8,128)}, f32[16,128]{1,0:T(8,128)}) custom-call(f32[512,4,4,512]{3,2,1,0:T(4,128)} %refs_0_.1, bf16[64,512,512]{2,1,0:T(8,128)(2,1)} %refs_1_.1, bf16[512,512]{1,0:T(8,128)(2,1)} %bitcast.8, bf16[256,64]{1,0:T(8,128)(2,1)} %bitcast.9), custom_call_target="tpu_custom_call" | custom-call | tf_op jit(solution)/shard_map/pallas_call | solution.py:493
  222.1 1.3 slice_reduce_fusion
  223.5 2.2 copy.8
